TPU v7x, 8 devices: a whole 2x2x1 slice. The times are simulated.
8 devices in a mesh: dp: 2 (over z, y), tp: 4 (over x, core).
Axes of the slice: x: 2, y: 2, z: 1, core: 2. Of those that a mesh axis runs over, the one named last changes fastest.
Arguments:
- x_tokens: bfloat16 [12, 64, 4096], P('dp', 'tp'), parts along dimension 0
- start_pos: int32 [12], P('dp'), parts along dimension 0
- k_cache: bfloat16 [2, 12, 8, 3136, 128], P(None, 'dp', 'tp'), parts along dimension 1
- v_cache: bfloat16 [2, 12, 8, 3136, 128], P(None, 'dp', 'tp'), parts along dimension 1
- w_q: bfloat16 [2, 4096, 6144], P(None, None, 'tp')
- w_k: bfloat16 [2, 4096, 1024], P(None, None, 'tp')
- w_v: bfloat16 [2, 4096, 1024], P(None, None, 'tp')
- w_o: bfloat16 [2, 6144, 4096], P(None, 'tp')
- w_up: bfloat16 [2, 4096, 16384], P(None, None, 'tp')
- w_down: bfloat16 [2, 16384, 4096], P(None, 'tp')
- ln_gain: bfloat16 [2, 2, 4096], replicated
- ln_bias: bfloat16 [2, 2, 4096], replicated
Outputs:
- output 1: bfloat16 [12, 64, 4096], P('dp', 'tp'), parts along dimension 0
- output 2: bfloat16 [2, 12, 8, 3136, 128], P(None, 'dp', 'tp'), parts along dimension 1
- output 3: bfloat16 [2, 12, 8, 3136, 128], P(None, 'dp', 'tp'), parts along dimension 1
There are 2 independent parts. A program takes and returns all parts, laid end to end along the dimension named above; an argument that names none is the same for every part.
All inputs are finite; a program needn't handle non-finite values.
Results may differ from a plain program's by a relative error of at most 0.0189325.
Values are sent between devices in bfloat16 or wider.
A program may use at most 1.25 GiB of HBM per device.

v0:
```python
import functools
import math

import jax
import jax.numpy as jnp
from jax import lax
from jax.experimental import pallas as pl
from jax.experimental.pallas import tpu as pltpu
from jax.sharding import PartitionSpec as P

LN_EPS = 1e-5
ROPE_BASE = 10000.0
NEG_BIG = -1e30
MIN_START = 768
BF = jnp.bfloat16
F32 = jnp.float32


def rope_tables(positions, head_dim):
    rot = head_dim // 2
    half = rot // 2
    lane = jnp.arange(head_dim, dtype=jnp.int32)
    freq = ROPE_BASE ** (-((lane % half).astype(F32) * (2.0 / rot)))
    angles = positions.astype(F32)[:, None] * freq
    cos_a, sin_a = jnp.cos(angles), jnp.sin(angles)
    c_tab = jnp.where(lane < rot, cos_a, 1.0)
    s_up = jnp.where((lane >= half) & (lane < rot), sin_a, 0.0)
    s_dn = jnp.where(lane < half, -sin_a, 0.0)
    return jnp.stack([c_tab, s_up, s_dn])


def attn_kernel(layer, dims, start_ref, q_ref, k_ref, v_ref, tab_ref, kc_hbm, vc_hbm, *rest):
    kv, group, toks, hd, s_len, ch, n_ch = dims
    if layer > 0:
        rest = rest[2:]
    ctx_ref, ko_hbm, vo_hbm, kbuf, vbuf, sbuf, ebuf, qbuf, mbuf, pbuf, lbuf, abuf, in_sem, out_sem = rest
    b = pl.program_id(0)
    nb = pl.num_programs(0)
    slot = lax.rem(b, 2)
    other = 1 - slot
    s_pad = kbuf.shape[2]
    win = toks + 16
    rows = group * toks
    coef = (hd ** -0.5) * math.log2(math.e)

    def load(bb, sl, go):
        for i, (src, dst) in enumerate(((kc_hbm, kbuf), (vc_hbm, vbuf))):
            copy = pltpu.make_async_copy(src.at[layer, bb], dst.at[sl, :, pl.ds(0, s_len), :], in_sem.at[sl, i])
            copy.start() if go else copy.wait()

    def save(bb, sl, go):
        for i, (src, dst) in enumerate(((kbuf, ko_hbm), (vbuf, vo_hbm))):
            copy = pltpu.make_async_copy(src.at[sl, :, pl.ds(0, s_len), :], dst.at[layer, bb], out_sem.at[sl, i])
            copy.start() if go else copy.wait()

    @pl.when(b == 0)
    def _():
        load(b, slot, True)
        if s_pad > s_len:
            for sl in range(2):
                kbuf[sl, :, s_len:, :] = jnp.zeros((kv, s_pad - s_len, hd), BF)
                vbuf[sl, :, s_len:, :] = jnp.zeros((kv, s_pad - s_len, hd), BF)

    @pl.when(b > 0)
    def _():
        save(b - 1, other, False)

    @pl.when(b + 1 < nb)
    def _():
        load(b + 1, other, True)

    c_tab, s_up, s_dn = tab_ref[0], tab_ref[1], tab_ref[2]
    half = hd // 4

    def rope(x):
        return x * c_tab + pltpu.roll(x, half, 1) * s_up + pltpu.roll(x, hd - half, 1) * s_dn

    for h in range(kv):
        for g in range(group):
            j = h * group + g
            qbuf[h, g * toks:(g + 1) * toks, :] = rope(q_ref[:, j * hd:(j + 1) * hd]).astype(BF)

    start = start_ref[b]
    base = jnp.minimum((start // 16) * 16, s_len - win)
    shift = start - base
    base = pl.multiple_of(base, 16)
    row_id = lax.broadcasted_iota(jnp.int32, (win, hd), 0)
    is_new = jnp.logical_and(row_id >= shift, row_id < shift + toks)

    load(b, slot, False)
    for h in range(kv):
        cols = slice(h * hd, (h + 1) * hd)
        for buf, fresh in ((kbuf, rope(k_ref[:, cols])), (vbuf, v_ref[:, cols])):
            fresh = fresh.astype(BF).astype(F32)
            fresh = jnp.concatenate([fresh, jnp.zeros((16, hd), F32)], axis=0)
            fresh = pltpu.roll(fresh, shift, 0)
            old = buf[slot, h, pl.ds(base, win), :].astype(F32)
            buf[slot, h, pl.ds(base, win), :] = jnp.where(is_new, fresh, old).astype(BF)
    save(b, slot, True)

    lbuf[...] = jnp.zeros(lbuf.shape, F32)
    abuf[...] = jnp.zeros(abuf.shape, F32)
    n_full = jnp.maximum(start // ch, 1)
    n_used = (start + toks + ch - 1) // ch
    step_rows = 64
    blocks = [slice(r, r + step_rows) for r in range(0, ch, step_rows)]
    ahead = lax.broadcasted_iota(jnp.int32, (step_rows, rows), 0) - lax.rem(lax.broadcasted_iota(jnp.int32, (step_rows, rows), 1), toks)

    def chunk(j):
        return pl.ds(pl.multiple_of(j * ch, ch), ch)

    def score(h, j):
        sbuf[h] = lax.dot_general(kbuf[slot, h, chunk(j), :], qbuf[h], (((1,), (1,)), ((), ())), preferred_element_type=F32)

    def scored(h, j, rb, masked):
        s = sbuf[h, rb]
        if masked:
            s = jnp.where(ahead <= start - j * ch - rb.start, s, NEG_BIG)
        return s.reshape(step_rows // 8, 8, rows)

    def peaks(h, j, masked):
        top = jnp.max(scored(h, j, blocks[0], masked), axis=0)
        for rb in blocks[1:]:
            top = jnp.maximum(top, jnp.max(scored(h, j, rb, masked), axis=0))
        peak = pbuf[h]
        mbuf[h] = peak
        pbuf[h] = jnp.maximum(peak, jnp.max(top, axis=0, keepdims=True))

    def weigh(h, j, masked):
        peak = pbuf[h]
        total = lbuf[h] * jnp.exp2((mbuf[h] - peak) * coef)
        for rb in blocks:
            e = jnp.exp2((scored(h, j, rb, masked) - peak) * coef)
            total = total + jnp.sum(e, axis=0)
            ebuf[h, rb] = e.reshape(step_rows, rows).astype(BF)
        lbuf[h] = total

    def mix(h, j, alpha):
        fresh = lax.dot_general(vbuf[slot, h, chunk(j), :], ebuf[h], (((0,), (0,)), ((), ())), preferred_element_type=F32)
        abuf[h] = (abuf[h].reshape(hd // 8, 8, rows) * alpha).reshape(hd, rows) + fresh

    def rescale(h):
        return jnp.exp2((mbuf[h] - pbuf[h]) * coef)

    def step(masked_now, masked_next, j, carry):
        for h in range(kv):
            alpha = rescale(h)
            weigh(h, j, masked_now)
            score(h, j + 1)
            mix(h, j, alpha)
        for h in range(kv):
            peaks(h, j + 1, masked_next)
        return carry

    pbuf[...] = jnp.full(pbuf.shape, NEG_BIG, F32)
    for h in range(kv):
        score(h, 0)
    for h in range(kv):
        peaks(h, 0, ch > MIN_START)
    last = n_used - 1
    lax.fori_loop(0, n_full - 1, functools.partial(step, ch > MIN_START, False), 0)
    lax.fori_loop(n_full - 1, last, functools.partial(step, True, True), 0)
    for h in range(kv):
        alpha = rescale(h)
        weigh(h, last, True)
        mix(h, last, alpha)
    for h in range(kv):
        ctx = (abuf[h] / jnp.sum(lbuf[h], axis=0, keepdims=True)).T.astype(BF)
        for g in range(group):
            j = h * group + g
            ctx_ref[:, j * hd:(j + 1) * hd] = ctx[g * toks:(g + 1) * toks, :]

    @pl.when(b == nb - 1)
    def _():
        save(b, slot, False)


def attend(layer, qkv, tabs, start_pos, k_cache, v_cache, prev):
    n_seq = start_pos.shape[0]
    _, _, kv, s_len, hd = k_cache.shape
    toks = qkv.shape[0] // n_seq
    kv_width = kv * hd
    q_width = qkv.shape[1] - 2 * kv_width
    group = q_width // kv_width
    n_ch = -(-s_len // 640)
    ch = 128 * -(-s_len // (128 * n_ch))
    rows = group * toks
    dims = (kv, group, toks, hd, s_len, ch, n_ch)
    any_spec = pl.BlockSpec(memory_space=pl.ANY)
    row_map = lambda b, *_: (b, 0)
    cache_shape = jax.ShapeDtypeStruct(k_cache.shape, BF)
    args = [start_pos, qkv, qkv, qkv, tabs, k_cache, v_cache] + list(prev)
    return pl.pallas_call(
        functools.partial(attn_kernel, layer, dims),
        grid_spec=pltpu.PrefetchScalarGridSpec(
            num_scalar_prefetch=1,
            grid=(n_seq,),
            in_specs=[
                pl.BlockSpec((toks, q_width), row_map),
                pl.BlockSpec((toks, kv_width), lambda b, *_: (b, group)),
                pl.BlockSpec((toks, kv_width), lambda b, *_: (b, group + 1)),
                pl.BlockSpec((3, toks, hd), lambda b, *_: (0, b, 0)),
            ] + [any_spec] * (2 + len(prev)),
            out_specs=[pl.BlockSpec((toks, q_width), row_map), any_spec, any_spec],
            scratch_shapes=[
                pltpu.VMEM((2, kv, ch * n_ch, hd), BF),
                pltpu.VMEM((2, kv, ch * n_ch, hd), BF),
                pltpu.VMEM((kv, ch, rows), F32),
                pltpu.VMEM((kv, ch, rows), BF),
                pltpu.VMEM((kv, rows, hd), BF),
                pltpu.VMEM((kv, 8, rows), F32),
                pltpu.VMEM((kv, 8, rows), F32),
                pltpu.VMEM((kv, 8, rows), F32),
                pltpu.VMEM((kv, hd, rows), F32),
                pltpu.SemaphoreType.DMA((2, 2)),
                pltpu.SemaphoreType.DMA((2, 2)),
            ],
        ),
        out_shape=[jax.ShapeDtypeStruct((n_seq * toks, q_width), BF), cache_shape, cache_shape],
        input_output_aliases={7: 1, 8: 2} if prev else {},
        compiler_params=pltpu.CompilerParams(vmem_limit_bytes=60 * 1024 * 1024, dimension_semantics=("arbitrary",)),
        cost_estimate=pl.CostEstimate(flops=8_000_000_000, bytes_accessed=80_000_000, transcendentals=15_000_000),
        name="attend",
    )(*args)


STEPS = 8
AHEAD = 3
EARLY = 2


def exchange_kernel(cfg, *args):
    refs = dict(zip(cfg['names'], args))
    layer, g_layer, ln_row = cfg['layer'], cfg['g_layer'], cfg['ln_row']
    scatter, gather = cfg['scatter'], cfg['gather']
    n_seq, toks, d_model = cfg['n_seq'], cfg['toks'], cfg['d_model']
    rows = n_seq * toks
    blk = d_model // STEPS
    me = lax.axis_index('tp')
    core = lax.rem(me, 2)
    partner = me + 1 - 2 * core
    counter = lax.rem(me + 2, 4)
    diag = lax.rem(partner + 2, 4)
    order = (me, partner, counter, diag)
    wbuf, xbuf = refs['wbuf'], refs['xbuf']

    barrier = pltpu.get_barrier_semaphore()
    for peer in (partner, counter):
        pl.semaphore_signal(barrier, inc=1, device_id={'tp': peer}, device_id_type=pl.DeviceIdType.MESH)

    def col(n, width=blk):
        return pl.ds(pl.multiple_of(n * width, width), width)

    x_copy = pltpu.make_async_copy(refs['x_hbm'], xbuf, refs['x_sem'])

    if scatter:
        depth = cfg['depth']
        abuf, w_s = refs['abuf'], refs['w_s']
        a_copies = [pltpu.make_async_copy(refs['a_hbm'].at[:, order[g]], abuf.at[g], refs['a_sem'].at[g]) for g in range(4)]

        def w_copy(n):
            return pltpu.make_async_copy(w_s.at[layer, :, col(n)], wbuf.at[pl.ds(0, depth), col(n)], refs['sw_sem'].at[n])

        for g in (2, 3):
            a_copies[g].start()
        w_copy(0).start()
        for g in (0, 1):
            a_copies[g].start()
        for n in range(1, AHEAD):
            w_copy(n).start()
    x_copy.start()

    g_copies = []
    if gather:
        if cfg['kind'] == 'up':
            cut = depth
            for i, (lo, hi) in enumerate(((cut, d_model), (0, cut))):
                span = pl.ds(lo, hi - lo)
                g_copies.append(pltpu.make_async_copy(refs['w_up'].at[g_layer, span, :], wbuf.at[span, :], refs['gw_sem'].at[i]))
        else:
            at = 0
            for i, name in enumerate(('w_q', 'w_k', 'w_v')):
                width = refs[name].shape[2]
                g_copies.append(pltpu.make_async_copy(refs[name].at[g_layer], wbuf.at[:, pl.ds(at, width)], refs['gw_sem'].at[i]))
                at += width

    def remote(src, dst, send, recv, peer):
        return pltpu.make_async_remote_copy(src_ref=src, dst_ref=dst, send_sem=send, recv_sem=recv, device_id={'tp': peer}, device_id_type=pl.DeviceIdType.MESH)

    if not scatter:
        x_copy.wait()
        for copy in g_copies:
            copy.start()
    pl.semaphore_wait(barrier, 2)

    if scatter:
        dsend, drecv, qsend, qrecv, own = refs['dsend'], refs['drecv'], refs['qsend'], refs['qrecv'], refs['own']
        part = refs['part']

        def d_copy(n, i):
            return remote(dsend.at[n, i], drecv.at[n, i], refs['ds_sem'].at[n, i], refs['dr_sem'].at[n, i], partner)

        def q_copy(n):
            return remote(qsend.at[n], qrecv.at[n], refs['qs_sem'].at[n], refs['qr_sem'].at[n], counter)

        for copy in a_copies:
            copy.wait()

        def s_step(n, carry):
            @pl.when(n + AHEAD < STEPS)
            def _():
                w_copy(n + AHEAD).start()

            w_copy(n).wait()
            far = jnp.dot(abuf[2:4].reshape(2 * rows, depth), wbuf[0:depth, col(n)], preferred_element_type=F32)
            dsend[n, 0] = far[rows:].astype(BF)
            d_copy(n, 0).start()
            part[...] = far[:rows]
            near = jnp.dot(abuf[0:2].reshape(2 * rows, depth), wbuf[0:depth, col(n)], preferred_element_type=F32)
            dsend[n, 1] = near[rows:].astype(BF)
            d_copy(n, 1).start()
            own[n] = near[:rows]
            d_copy(n, 0).wait_recv()
            qsend[n] = (part[...] + drecv[n, 0].astype(F32)).astype(BF)
            q_copy(n).start()
            return carry

        half = STEPS - AHEAD
        lax.fori_loop(0, half, s_step, 0)
        if gather:
            for copy in g_copies[:1] if cfg['kind'] == 'up' else g_copies:
                copy.start()
        lax.fori_loop(half, STEPS, s_step, 0)
        if gather and cfg['kind'] == 'up':
            g_copies[1].start()
        x_copy.wait()

    if gather:
        near_h, far_x, far_h, acc, stage, y_out = (refs[k] for k in ('near_h', 'far_x', 'far_h', 'acc', 'stage', 'y_out'))
        stat, far_stat = refs['stat'], refs['far_stat']
        n_out = acc.shape[1]

        def c_copy(k):
            return remote(xbuf.at[:, col(k)], far_x.at[pl.ds(0, rows), col(k)], refs['cs_sem'].at[k], refs['cr_sem'].at[k], counter)

        def f_copy(k):
            return remote(far_x.at[pl.ds(0, rows), col(k)], far_x.at[pl.ds(rows, rows), col(k)], refs['fs_sem'].at[k], refs['fr_sem'].at[k], partner)

        def p_copy(k):
            return remote(near_h.at[pl.ds(0, rows), col(k)], near_h.at[pl.ds(rows, rows), col(k)], refs['ps_sem'].at[k], refs['pr_sem'].at[k], partner)

        stat_copy = remote(stat, far_stat.at[0], refs['ts_sem'].at[0], refs['tr_sem'].at[0], counter)
        stat_pass = remote(far_stat.at[0], far_stat.at[1], refs['ts_sem'].at[1], refs['tr_sem'].at[1], partner)

    total = jnp.zeros((rows, 128), F32)
    for n in range(STEPS):
        cols = slice(n * blk, (n + 1) * blk)
        if scatter:
            d_copy(n, 1).wait_recv()
            q_copy(n).wait_recv()
            summed = own[n] + drecv[n, 1].astype(F32) + qrecv[n].astype(F32)
            fresh = (xbuf[:, cols].astype(F32) + summed.astype(BF).astype(F32)).astype(BF)
            xbuf[:, cols] = fresh
        else:
            fresh = xbuf[:, cols]
        if gather and 1 <= n <= EARLY:
            c_copy(n - 1).start()
        fresh = fresh.astype(F32)
        for j in range(blk // 128):
            total = total + fresh[:, j * 128:(j + 1) * 128]
    if scatter:
        out_copy = pltpu.make_async_copy(xbuf, refs['x_out'], refs['x_sem'])
        out_copy.start()

    if gather:
        mean = jnp.sum(total, axis=-1, keepdims=True) / d_model
        total = jnp.zeros((rows, 128), F32)
        for n in range(STEPS):
            diff = xbuf[:, n * blk:(n + 1) * blk].astype(F32) - mean
            diff = diff * diff
            for j in range(blk // 128):
                total = total + diff[:, j * 128:(j + 1) * 128]
        inv = lax.rsqrt(jnp.sum(total, axis=-1, keepdims=True) / d_model + LN_EPS)
        stat[...] = jnp.where(lax.broadcasted_iota(jnp.int32, (rows, 128), 1) < 64, mean, inv)

        def norm(values, mean, inv, cols):
            gain = refs['ln_gain'][ln_row // 2, ln_row % 2:ln_row % 2 + 1, cols].astype(F32)
            bias = refs['ln_bias'][ln_row // 2, ln_row % 2:ln_row % 2 + 1, cols].astype(F32)
            return ((values.astype(F32) - mean) * inv * (1.0 + gain) + bias).astype(BF)

        for k in range(STEPS):
            cols = slice(k * blk, (k + 1) * blk)
            near_h[0:rows, cols] = norm(xbuf[:, cols], mean, inv, cols)
            if k == 0:
                stat_copy.start()
                for n in range(EARLY, STEPS):
                    c_copy(n).start()
            else:
                p_copy(k - 1).start()
        acc[...] = jnp.zeros(acc.shape, F32)
        p_copy(STEPS - 1).start()

        for copy in g_copies:
            copy.wait()
        for k in range(STEPS):
            p_copy(k).wait_recv()

        def finish(value):
            if cfg['kind'] == 'up':
                value = jnp.square(jnp.maximum(value, 0.0)).astype(BF)
            return value.reshape(2, n_seq, toks, value.shape[-1])

        n_blk = n_out // STEPS

        def y_copy(g, n):
            return pltpu.make_async_copy(stage.at[g, :, :, col(n, n_blk)], y_out.at[:, order[g], :, col(n, n_blk)], refs['y_sem'].at[g, n])

        piece = min(1024, n_out)

        def far_norm(k):
            f_copy(k).wait_recv()
            for r in range(2):
                part_rows = slice(r * rows, (r + 1) * rows)
                far_h[part_rows] = norm(far_x[part_rows, col(k)], far_stat[r, :, 0:1], far_stat[r, :, 64:65], col(k))

        def far_dot(k, cols):
            return jnp.dot(far_h[...], wbuf[col(k), cols], preferred_element_type=F32)

        def near_step(i):
            near = jnp.dot(near_h[...], wbuf[:, col(i, n_blk)], preferred_element_type=F32)
            stage[0:2, :, :, col(i, n_blk)] = finish(near)
            y_copy(0, i).start()
            y_copy(1, i).start()
            c_copy(i).wait_recv()
            f_copy(i).start()

        def g_step(i, carry):
            near_step(i)
            far_norm(i - 1)
            for n in range(n_out // piece):
                cols = slice(n * piece, (n + 1) * piece)
                acc[:, cols] += far_dot(i - 1, cols)
            return carry

        near_step(0)
        stat_copy.wait_recv()
        stat_pass.start()
        stat_pass.wait_recv()
        lax.fori_loop(1, STEPS, g_step, 0)
        far_norm(STEPS - 1)
        for n in range(n_out // piece):
            cols = slice(n * piece, (n + 1) * piece)
            stage[2:4, :, :, cols] = finish(acc[:, cols] + far_dot(STEPS - 1, cols))
            for m in range(n * piece // n_blk, (n + 1) * piece // n_blk):
                y_copy(2, m).start()
                y_copy(3, m).start()
        stat_copy.wait_send()
        stat_pass.wait_send()
        for k in range(STEPS):
            c_copy(k).wait_send()
            p_copy(k).wait_send()
            f_copy(k).wait_send()
            for g in range(4):
                y_copy(g, k).wait()

    if scatter:
        for n in range(STEPS):
            d_copy(n, 0).wait_send()
            d_copy(n, 1).wait_send()
            q_copy(n).wait_send()
        out_copy.wait()


def exchange(cid, x, ln_gain, ln_bias, *, n_seq, layer=0, a=None, w_s=None, g_layer=0, ln_row=0, kind=None, weights=()):
    rows, d_model = x.shape
    toks = rows // n_seq
    blk = d_model // STEPS
    scatter, gather = a is not None, kind is not None
    any_spec, vmem = pl.BlockSpec(memory_space=pl.ANY), pl.BlockSpec(memory_space=pltpu.VMEM)
    dma = pltpu.SemaphoreType.DMA
    ins, outs, scr = [('x_hbm', x, any_spec)], [], []
    flops, moved = 0, 4_000_000
    scr += [('wbuf', None), ('xbuf', pltpu.VMEM((rows, d_model), BF)), ('x_sem', dma)]
    width = 0
    if scatter:
        depth = a.shape[3]
        ins += [('a_hbm', a, any_spec), ('w_s', w_s, any_spec)]
        outs += [('x_out', jax.ShapeDtypeStruct(x.shape, BF))]
        scr += [
            ('abuf', pltpu.VMEM((4, n_seq, toks, depth), BF)), ('a_sem', dma((4,))), ('sw_sem', dma((STEPS,))),
            ('dsend', pltpu.VMEM((STEPS, 2, rows, blk), BF)), ('drecv', pltpu.VMEM((STEPS, 2, rows, blk), BF)),
            ('qsend', pltpu.VMEM((STEPS, rows, blk), BF)), ('qrecv', pltpu.VMEM((STEPS, rows, blk), BF)),
            ('own', pltpu.VMEM((STEPS, rows, blk), F32)), ('part', pltpu.VMEM((rows, blk), F32)),
            ('ds_sem', dma((STEPS, 2))), ('dr_sem', dma((STEPS, 2))), ('qs_sem', dma((STEPS,))), ('qr_sem', dma((STEPS,))),
        ]
        width = d_model
        w_rows = depth
        flops += 2 * 4 * rows * depth * d_model
        moved += depth * d_model * 2
    if gather:
        names = ('w_up',) if kind == 'up' else ('w_q', 'w_k', 'w_v')
        ins += list(zip(names, weights, [any_spec] * len(names)))
        ins += [('ln_gain', ln_gain, vmem), ('ln_bias', ln_bias, vmem)]
        n_out = sum(w.shape[2] for w in weights)
        y_type = BF if kind == 'up' else F32
        outs += [('y_out', jax.ShapeDtypeStruct((n_seq, 4, toks, n_out), y_type))]
        scr += [
            ('near_h', pltpu.VMEM((2 * rows, d_model), BF)), ('far_x', pltpu.VMEM((2 * rows, d_model), BF)),
            ('far_h', pltpu.VMEM((2 * rows, blk), BF)), ('stat', pltpu.VMEM((rows, 128), F32)), ('far_stat', pltpu.VMEM((2, rows, 128), F32)),
            ('ts_sem', dma((2,))), ('tr_sem', dma((2,))),
            ('acc', pltpu.VMEM((2 * rows, n_out), F32)), ('stage', pltpu.VMEM((4, n_seq, toks, n_out), y_type)),
            ('gw_sem', dma((3,))), ('y_sem', dma((4, STEPS))),
        ] + [(s, dma((STEPS,))) for s in ('cs_sem', 'cr_sem', 'fs_sem', 'fr_sem', 'ps_sem', 'pr_sem')]
        width = max(width, n_out)
        w_rows = d_model
        flops += 2 * 4 * rows * n_out * d_model
        moved += n_out * d_model * 2
    scr[0] = ('wbuf', pltpu.VMEM((w_rows, width), BF))
    cfg = dict(
        names=[i[0] for i in ins] + [o[0] for o in outs] + [s[0] for s in scr], layer=layer, g_layer=g_layer, ln_row=ln_row,
        scatter=scatter, gather=gather, n_seq=n_seq, toks=toks, d_model=d_model, kind=kind, depth=depth if scatter else 0,
    )
    return pl.pallas_call(
        functools.partial(exchange_kernel, cfg),
        in_specs=[i[2] for i in ins],
        out_specs=[any_spec] * len(outs),
        out_shape=[o[1] for o in outs],
        scratch_shapes=[s[1] for s in scr],
        compiler_params=pltpu.CompilerParams(collective_id=cid, has_side_effects=True, vmem_limit_bytes=66_000_000),
        cost_estimate=pl.CostEstimate(flops=flops, bytes_accessed=moved, transcendentals=0),
        name=('scatter_' if scatter else '') + ('gather_' + kind if gather else 'end'),
    )(*[i[1] for i in ins])


def solution(mesh):
    tok_spec = P('dp', 'tp', None)
    cache_spec = P(None, 'dp', 'tp', None, None)
    col_spec = P(None, None, 'tp')
    row_spec = P(None, 'tp', None)

    def device_fn(x_loc, start_pos, k_cache, v_cache, w_q, w_k, w_v, w_o, w_up, w_down, ln_gain, ln_bias):
        n_layers = w_q.shape[0]
        n_seq, tok_loc, d_model = x_loc.shape
        new_len = tok_loc * 4
        rows = n_seq * new_len
        positions = (start_pos[:, None] + jnp.arange(new_len, dtype=jnp.int32)[None, :]).reshape(rows)
        tabs = rope_tables(positions, k_cache.shape[4])
        gain, bias = ln_gain, ln_bias
        hidden = x_loc.reshape(n_seq * tok_loc, d_model)
        prev = ()
        qkv, = exchange(0, hidden, gain, bias, n_seq=n_seq, kind='qkv', weights=(w_q, w_k, w_v))
        for layer in range(n_layers):
            context, *prev = attend(layer, qkv.reshape(rows, -1), tabs, start_pos, k_cache, v_cache, prev)
            context = context.reshape(n_seq, 4, tok_loc, -1)
            hidden, act = exchange(2 * layer + 1, hidden, gain, bias, n_seq=n_seq, layer=layer, a=context, w_s=w_o, g_layer=layer, ln_row=2 * layer + 1, kind='up', weights=(w_up,))
            if layer + 1 < n_layers:
                hidden, qkv = exchange(2 * layer + 2, hidden, gain, bias, n_seq=n_seq, layer=layer, a=act, w_s=w_down, g_layer=layer + 1, ln_row=2 * layer + 2, kind='qkv', weights=(w_q, w_k, w_v))
            else:
                hidden, = exchange(2 * layer + 2, hidden, gain, bias, n_seq=n_seq, layer=layer, a=act, w_s=w_down)
        return hidden.reshape(x_loc.shape), prev[0], prev[1]

    return jax.shard_map(device_fn, mesh=mesh, in_specs=(tok_spec, P('dp'), cache_spec, cache_spec, col_spec, col_spec, col_spec, row_spec, col_spec, row_spec, P(), P()), out_specs=(tok_spec, cache_spec, cache_spec), check_vma=False)
```

profile of v0, /device:TPU:0, one launch (start us, length us, event | category | flops | bytes accessed | tf_op | source)
XLA Modules:
  0.0 261.0 jit_solution(2612824610925099073)
XLA Ops:
  0.7 0.7 add_convert_fusion
  1.4 0.1 convert_element_type.18
  1.5 0.8 fusion.3
  2.3 0.9 pad_maximum_fusion.tab_ref
  3.1 29.6 %gather_qkv.1 = f32[6,4,16,2048]{3,2,1,0:T(8,128)} custom-call(bf16[96,4096]{1,0:T(8,128)(2,1)} %bitcast.13, bf16[2,4096,1536]{2,1,0:T(8,128)(2,1)} %args_3_.9, bf16[2,4096,256]{2,1,0:T(8,128)(2,1)} %args_4_.9, bf16[2,4096,256]{2,1,0:T(8,128)(2,1)} %args_5_.9, bf16[2,2,4096]{2,1,0:T(2,128)(2,1)} %args_4_.10, bf16[2,2,4096]{2,1,0:T(2,128)(2,1)} %args_5_.10), custom_call_target="tpu_custom_call" | custom-call | flops 6442450944 | bytes 20777216 | tf_op jit(solution)/shard_map/gather_qkv/pallas_call | solution.py:523
  32.7 26.4 %attend.2 = (bf16[384,1536]{1,0:T(8,128)(2,1)}, bf16[2,6,2,3136,128]{4,3,2,1,0:T(8,128)(2,1)}, bf16[2,6,2,3136,128]{4,3,2,1,0:T(8,128)(2,1)}) custom-call(s32[6]{0:T(128)} %start_ref.3, f32[384,2048]{1,0:T(8,128)} %bitcast.6, f32[384,2048]{1,0:T(8,128)} %bitcast.7, f32[384,2048]{1,0:T(8,128)} %bitcast.8, f32[3,384,128]{2,1,0:T(8,128)} %pad_maximum_fusion.tab_ref, ...), custom_call_target="tpu_custom_call" | custom-call | flops 8000000000 | bytes 80000000 | tf_op jit(solution)/shard_map/attend/pallas_call | solution.py:193
  59.2 48.2 %scatter_gather_up.2 = (bf16[96,4096]{1,0:T(8,128)(2,1)}, bf16[6,4,16,4096]{3,2,1,0:T(8,128)(2,1)}) custom-call(bf16[96,4096]{1,0:T(8,128)(2,1)} %bitcast.14, bf16[6,4,16,1536]{3,2,1,0:T(8,128)(2,1)} %bitcast.16, bf16[2,1536,4096]{2,1,0:T(8,128)(2,1)} %args_2_.11, bf16[2,4096,4096]{2,1,0:T(8,128)(2,1)} %args_3_.10, bf16[2,2,4096]{2,1,0:T(2,128)(2,1)} %args_4_.10, ...), custom_call_target="tpu_custom_call" | custom-call | flops 17716740096 | bytes 50137344 | tf_op jit(solution)/shard_map/scatter_gather_up/pallas_call | solution.py:523
  107.4 49.8 %scatter_gather_qkv.1 = (bf16[96,4096]{1,0:T(8,128)(2,1)}, f32[6,4,16,2048]{3,2,1,0:T(8,128)}) custom-call(bf16[96,4096]{1,0:T(8,128)(2,1)} %get-tuple-element.16.args_0_, bf16[6,4,16,4096]{3,2,1,0:T(8,128)(2,1)} %get-tuple-element.17.args_1_, bf16[2,4096,4096]{2,1,0:T(8,128)(2,1)} %args_2_.12, bf16[2,4096,1536]{2,1,0:T(8,128)(2,1)} %args_3_.9, ...), custom_call_target="tpu_custom_call" | custom-call | flops 19327352832 | bytes 54331648 | tf_op jit(solution)/shard_map/scatter_gather_qkv/pallas_call | solution.py:523
  157.2 26.5 %attend.3 = (bf16[384,1536]{1,0:T(8,128)(2,1)}, bf16[2,6,2,3136,128]{4,3,2,1,0:T(8,128)(2,1)}, bf16[2,6,2,3136,128]{4,3,2,1,0:T(8,128)(2,1)}) custom-call(s32[6]{0:T(128)} %start_ref.3, f32[384,2048]{1,0:T(8,128)} %bitcast.9, f32[384,2048]{1,0:T(8,128)} %bitcast.10, f32[384,2048]{1,0:T(8,128)} %bitcast.11, ...), custom_call_target="tpu_custom_call", output_to_operand_aliasing={{1}: (7, {}), {2}: (8, {})} | custom-call | flops 8000000000 | bytes 80000000 | tf_op jit(solution)/shard_map/attend/pallas_call | solution.py:193
  183.7 48.3 %scatter_gather_up.3 = (bf16[96,4096]{1,0:T(8,128)(2,1)}, bf16[6,4,16,4096]{3,2,1,0:T(8,128)(2,1)}) custom-call(bf16[96,4096]{1,0:T(8,128)(2,1)} %get-tuple-element.18.args_0_, bf16[6,4,16,1536]{3,2,1,0:T(8,128)(2,1)} %bitcast.15, bf16[2,1536,4096]{2,1,0:T(8,128)(2,1)} %args_2_.11, bf16[2,4096,4096]{2,1,0:T(8,128)(2,1)} %args_3_.10, ...), custom_call_target="tpu_custom_call" | custom-call | flops 17716740096 | bytes 50137344 | tf_op jit(solution)/shard_map/scatter_gather_up/pallas_call | solution.py:523
  232.0 26.9 %scatter_end.1 = bf16[96,4096]{1,0:T(8,128)(2,1)} custom-call(bf16[96,4096]{1,0:T(8,128)(2,1)} %get-tuple-element.23.args_0_, bf16[6,4,16,4096]{3,2,1,0:T(8,128)(2,1)} %get-tuple-element.24.args_1_, bf16[2,4096,4096]{2,1,0:T(8,128)(2,1)} %args_2_.12), custom_call_target="tpu_custom_call" | custom-call | flops 12884901888 | bytes 37554432 | tf_op jit(solution)/shard_map/scatter_end/pallas_call | solution.py:523
  258.9 2.1 copy.20
  (3 shorter events, 0.0 us)
where the time goes:
time: 263 us; the launch traced here: 261 us
  Pallas kernels  256 us (97%)
    pallas_call x5, Pallas kernels, exchange(): pl.pallas_call(functools.partial(exchange_kernel, cfg), in_specs=[i[2] fo...  203 us
    pallas_call x2, Pallas kernels, attend(): pl.pallas_call(functools.partial(attn_kernel, layer, dims), grid_spec=plt...  52.9 us

commit v1 on v0

v1 whole, which is shorter than its diff:
```python
import functools
import math

import jax
import jax.numpy as jnp
from jax import lax
from jax.experimental import pallas as pl
from jax.experimental.pallas import tpu as pltpu
from jax.sharding import PartitionSpec as P

LN_EPS = 1e-5
ROPE_BASE = 10000.0
NEG_BIG = -1e30
MIN_START = 768
BF = jnp.bfloat16
F32 = jnp.float32


def rope_tables(positions, head_dim):
    rot = head_dim // 2
    half = rot // 2
    lane = jnp.arange(head_dim, dtype=jnp.int32)
    freq = ROPE_BASE ** (-((lane % half).astype(F32) * (2.0 / rot)))
    angles = positions.astype(F32)[:, None] * freq
    cos_a, sin_a = jnp.cos(angles), jnp.sin(angles)
    c_tab = jnp.where(lane < rot, cos_a, 1.0)
    s_up = jnp.where((lane >= half) & (lane < rot), sin_a, 0.0)
    s_dn = jnp.where(lane < half, -sin_a, 0.0)
    return jnp.stack([c_tab, s_up, s_dn])


def attn_kernel(layer, dims, start_ref, q_ref, k_ref, v_ref, tab_ref, kc_hbm, vc_hbm, *rest):
    kv, group, toks, hd, s_len, ch, n_ch = dims
    if layer > 0:
        rest = rest[2:]
    ctx_ref, ko_hbm, vo_hbm, kbuf, vbuf, sbuf, ebuf, qbuf, mbuf, pbuf, lbuf, abuf, in_sem, out_sem = rest
    b = pl.program_id(0)
    nb = pl.num_programs(0)
    slot = lax.rem(b, 2)
    other = 1 - slot
    s_pad = kbuf.shape[2]
    win = toks + 16
    rows = group * toks
    coef = (hd ** -0.5) * math.log2(math.e)

    def load(bb, sl, go):
        for i, (src, dst) in enumerate(((kc_hbm, kbuf), (vc_hbm, vbuf))):
            copy = pltpu.make_async_copy(src.at[layer, bb], dst.at[sl, :, pl.ds(0, s_len), :], in_sem.at[sl, i])
            copy.start() if go else copy.wait()

    def save(bb, sl, go):
        for i, (src, dst) in enumerate(((kbuf, ko_hbm), (vbuf, vo_hbm))):
            copy = pltpu.make_async_copy(src.at[sl, :, pl.ds(0, s_len), :], dst.at[layer, bb], out_sem.at[sl, i])
            copy.start() if go else copy.wait()

    @pl.when(b == 0)
    def _():
        load(b, slot, True)
        if s_pad > s_len:
            for sl in range(2):
                kbuf[sl, :, s_len:, :] = jnp.zeros((kv, s_pad - s_len, hd), BF)
                vbuf[sl, :, s_len:, :] = jnp.zeros((kv, s_pad - s_len, hd), BF)

    @pl.when(b > 0)
    def _():
        save(b - 1, other, False)

    @pl.when(b + 1 < nb)
    def _():
        load(b + 1, other, True)

    c_tab, s_up, s_dn = tab_ref[0], tab_ref[1], tab_ref[2]
    half = hd // 4

    def rope(x):
        return x * c_tab + pltpu.roll(x, half, 1) * s_up + pltpu.roll(x, hd - half, 1) * s_dn

    for h in range(kv):
        for g in range(group):
            j = h * group + g
            qbuf[h, g * toks:(g + 1) * toks, :] = rope(q_ref[:, j * hd:(j + 1) * hd]).astype(BF)

    start = start_ref[b]
    base = jnp.minimum((start // 16) * 16, s_len - win)
    shift = start - base
    base = pl.multiple_of(base, 16)
    row_id = lax.broadcasted_iota(jnp.int32, (win, hd), 0)
    is_new = jnp.logical_and(row_id >= shift, row_id < shift + toks)

    load(b, slot, False)
    for h in range(kv):
        cols = slice(h * hd, (h + 1) * hd)
        for buf, fresh in ((kbuf, rope(k_ref[:, cols])), (vbuf, v_ref[:, cols])):
            fresh = fresh.astype(BF).astype(F32)
            fresh = jnp.concatenate([fresh, jnp.zeros((16, hd), F32)], axis=0)
            fresh = pltpu.roll(fresh, shift, 0)
            old = buf[slot, h, pl.ds(base, win), :].astype(F32)
            buf[slot, h, pl.ds(base, win), :] = jnp.where(is_new, fresh, old).astype(BF)
    save(b, slot, True)

    lbuf[...] = jnp.zeros(lbuf.shape, F32)
    abuf[...] = jnp.zeros(abuf.shape, F32)
    n_full = jnp.maximum(start // ch, 1)
    n_used = (start + toks + ch - 1) // ch
    step_rows = 64
    blocks = [slice(r, r + step_rows) for r in range(0, ch, step_rows)]
    ahead = lax.broadcasted_iota(jnp.int32, (step_rows, rows), 0) - lax.rem(lax.broadcasted_iota(jnp.int32, (step_rows, rows), 1), toks)

    def chunk(j):
        return pl.ds(pl.multiple_of(j * ch, ch), ch)

    def score(h, j):
        sbuf[h] = lax.dot_general(kbuf[slot, h, chunk(j), :], qbuf[h], (((1,), (1,)), ((), ())), preferred_element_type=F32)

    def scored(h, j, rb, masked):
        s = sbuf[h, rb]
        if masked:
            s = jnp.where(ahead <= start - j * ch - rb.start, s, NEG_BIG)
        return s.reshape(step_rows // 8, 8, rows)

    def peaks(h, j, masked):
        top = jnp.max(scored(h, j, blocks[0], masked), axis=0)
        for rb in blocks[1:]:
            top = jnp.maximum(top, jnp.max(scored(h, j, rb, masked), axis=0))
        peak = pbuf[h]
        mbuf[h] = peak
        pbuf[h] = jnp.maximum(peak, jnp.max(top, axis=0, keepdims=True))

    def weigh(h, j, masked):
        peak = pbuf[h]
        total = lbuf[h] * jnp.exp2((mbuf[h] - peak) * coef)
        for rb in blocks:
            e = jnp.exp2((scored(h, j, rb, masked) - peak) * coef)
            total = total + jnp.sum(e, axis=0)
            ebuf[h, rb] = e.reshape(step_rows, rows).astype(BF)
        lbuf[h] = total

    def mix(h, j, alpha):
        fresh = lax.dot_general(vbuf[slot, h, chunk(j), :], ebuf[h], (((0,), (0,)), ((), ())), preferred_element_type=F32)
        abuf[h] = (abuf[h].reshape(hd // 8, 8, rows) * alpha).reshape(hd, rows) + fresh

    def rescale(h):
        return jnp.exp2((mbuf[h] - pbuf[h]) * coef)

    def step(masked_now, masked_next, j, carry):
        for h in range(kv):
            alpha = rescale(h)
            weigh(h, j, masked_now)
            score(h, j + 1)
            mix(h, j, alpha)
        for h in range(kv):
            peaks(h, j + 1, masked_next)
        return carry

    pbuf[...] = jnp.full(pbuf.shape, NEG_BIG, F32)
    for h in range(kv):
        score(h, 0)
    for h in range(kv):
        peaks(h, 0, ch > MIN_START)
    last = n_used - 1
    lax.fori_loop(0, n_full - 1, functools.partial(step, ch > MIN_START, False), 0)
    lax.fori_loop(n_full - 1, last, functools.partial(step, True, True), 0)
    for h in range(kv):
        alpha = rescale(h)
        weigh(h, last, True)
        mix(h, last, alpha)
    for h in range(kv):
        ctx = (abuf[h] / jnp.sum(lbuf[h], axis=0, keepdims=True)).T.astype(BF)
        for g in range(group):
            j = h * group + g
            ctx_ref[:, j * hd:(j + 1) * hd] = ctx[g * toks:(g + 1) * toks, :]

    @pl.when(b == nb - 1)
    def _():
        save(b, slot, False)


def attend(layer, qkv, tabs, start_pos, k_cache, v_cache, prev):
    n_seq = start_pos.shape[0]
    _, _, kv, s_len, hd = k_cache.shape
    toks = qkv.shape[0] // n_seq
    kv_width = kv * hd
    q_width = qkv.shape[1] - 2 * kv_width
    group = q_width // kv_width
    n_ch = -(-s_len // 640)
    ch = 128 * -(-s_len // (128 * n_ch))
    rows = group * toks
    dims = (kv, group, toks, hd, s_len, ch, n_ch)
    any_spec = pl.BlockSpec(memory_space=pl.ANY)
    row_map = lambda b, *_: (b, 0)
    cache_shape = jax.ShapeDtypeStruct(k_cache.shape, BF)
    args = [start_pos, qkv, qkv, qkv, tabs, k_cache, v_cache] + list(prev)
    return pl.pallas_call(
        functools.partial(attn_kernel, layer, dims),
        grid_spec=pltpu.PrefetchScalarGridSpec(
            num_scalar_prefetch=1,
            grid=(n_seq,),
            in_specs=[
                pl.BlockSpec((toks, q_width), row_map),
                pl.BlockSpec((toks, kv_width), lambda b, *_: (b, group)),
                pl.BlockSpec((toks, kv_width), lambda b, *_: (b, group + 1)),
                pl.BlockSpec((3, toks, hd), lambda b, *_: (0, b, 0)),
            ] + [any_spec] * (2 + len(prev)),
            out_specs=[pl.BlockSpec((toks, q_width), row_map), any_spec, any_spec],
            scratch_shapes=[
                pltpu.VMEM((2, kv, ch * n_ch, hd), BF),
                pltpu.VMEM((2, kv, ch * n_ch, hd), BF),
                pltpu.VMEM((kv, ch, rows), F32),
                pltpu.VMEM((kv, ch, rows), BF),
                pltpu.VMEM((kv, rows, hd), BF),
                pltpu.VMEM((kv, 8, rows), F32),
                pltpu.VMEM((kv, 8, rows), F32),
                pltpu.VMEM((kv, 8, rows), F32),
                pltpu.VMEM((kv, hd, rows), F32),
                pltpu.SemaphoreType.DMA((2, 2)),
                pltpu.SemaphoreType.DMA((2, 2)),
            ],
        ),
        out_shape=[jax.ShapeDtypeStruct((n_seq * toks, q_width), BF), cache_shape, cache_shape],
        input_output_aliases={7: 1, 8: 2} if prev else {},
        compiler_params=pltpu.CompilerParams(vmem_limit_bytes=60 * 1024 * 1024, dimension_semantics=("arbitrary",)),
        cost_estimate=pl.CostEstimate(flops=8_000_000_000, bytes_accessed=80_000_000, transcendentals=15_000_000),
        name="attend",
    )(*args)


STEPS = 8
WIDE = STEPS + 2


def exchange_kernel(cfg, *args):
    refs = dict(zip(cfg['names'], args))
    n_seq, toks, d_model = cfg['n_seq'], cfg['toks'], cfg['d_model']
    rows = n_seq * toks
    blk = d_model // STEPS
    me = lax.axis_index('tp')
    core = lax.rem(me, 2)
    partner = me + 1 - 2 * core
    counter = lax.rem(me + 2, 4)
    diag = lax.rem(partner + 2, 4)
    order = (me, partner, counter, diag)
    wbuf, xbuf = refs['wbuf'], refs['xbuf']

    barrier = pltpu.get_barrier_semaphore()
    for peer in (partner, counter):
        pl.semaphore_signal(barrier, inc=1, device_id={'tp': peer}, device_id_type=pl.DeviceIdType.MESH)

    def col(n, width=blk):
        return pl.ds(pl.multiple_of(n * width, width), width)

    def remote(src, dst, send, recv, peer):
        return pltpu.make_async_remote_copy(src_ref=src, dst_ref=dst, send_sem=send, recv_sem=recv, device_id={'tp': peer}, device_id_type=pl.DeviceIdType.MESH)

    def fold(values, total):
        for j in range(blk // 128):
            total = total + values[:, j * 128:(j + 1) * 128]
        return total

    def scatter(tag, a_ref, w_copy, slot_of, depth, ahead, late):
        dsend, drecv, qsend, qrecv, own, part = (refs[k] for k in ('dsend', 'drecv', 'qsend', 'qrecv', 'own', 'part'))
        ds_sem, dr_sem, qs_sem, qr_sem = (refs[tag + k] for k in ('ds', 'dr', 'qs', 'qr'))

        def d_copy(n, i):
            return remote(dsend.at[n, i], drecv.at[n, i], ds_sem.at[n, i], dr_sem.at[n, i], partner)

        def q_copy(n):
            return remote(qsend.at[n], qrecv.at[n], qs_sem.at[n], qr_sem.at[n], counter)

        def step(n, carry):
            @pl.when(n + ahead < STEPS)
            def _():
                w_copy(n + ahead).start()

            w_copy(n).wait()
            cols = col(slot_of(n))
            far = jnp.dot(a_ref[2:4].reshape(2 * rows, depth), wbuf[0:depth, cols], preferred_element_type=F32)
            dsend[n, 0] = far[rows:].astype(BF)
            d_copy(n, 0).start()
            part[...] = far[:rows]
            near = jnp.dot(a_ref[0:2].reshape(2 * rows, depth), wbuf[0:depth, cols], preferred_element_type=F32)
            dsend[n, 1] = near[rows:].astype(BF)
            d_copy(n, 1).start()
            own[n] = near[:rows]
            d_copy(n, 0).wait_recv()
            qsend[n] = (part[...] + drecv[n, 0].astype(F32)).astype(BF)
            q_copy(n).start()
            return carry

        half = STEPS - 3
        lax.fori_loop(0, half, step, 0)
        late(0)
        lax.fori_loop(half, STEPS, step, 0)
        late(1)
        total = jnp.zeros((rows, 128), F32)
        for n in range(STEPS):
            cols = slice(n * blk, (n + 1) * blk)
            d_copy(n, 1).wait_recv()
            q_copy(n).wait_recv()
            summed = own[n] + drecv[n, 1].astype(F32) + qrecv[n].astype(F32)
            fresh = (xbuf[:, cols].astype(F32) + summed.astype(BF).astype(F32)).astype(BF)
            xbuf[:, cols] = fresh
            total = fold(fresh.astype(F32), total)
        for n in range(STEPS):
            d_copy(n, 0).wait_send()
            d_copy(n, 1).wait_send()
            q_copy(n).wait_send()
        return total

    def gather(tag, ln_row, total, w_at, n_out, ready, finish):
        near_h, far_h, acc = refs['near_h'], refs['far_h'], refs['acc']
        cs, cr, fs, fr, ps, pr = (refs[tag + k] for k in ('cs', 'cr', 'fs', 'fr', 'ps', 'pr'))
        mean = jnp.sum(total, axis=-1, keepdims=True) / d_model
        total = jnp.zeros((rows, 128), F32)
        for n in range(STEPS):
            diff = xbuf[:, n * blk:(n + 1) * blk].astype(F32) - mean
            total = fold(diff * diff, total)
        inv = lax.rsqrt(jnp.sum(total, axis=-1, keepdims=True) / d_model + LN_EPS)

        def c_copy(k):
            return remote(near_h.at[pl.ds(0, rows), col(k)], far_h.at[pl.ds(0, rows), col(k)], cs.at[k], cr.at[k], counter)

        def f_copy(k):
            return remote(far_h.at[pl.ds(0, rows), col(k)], far_h.at[pl.ds(rows, rows), col(k)], fs.at[k], fr.at[k], partner)

        def p_copy(k):
            return remote(near_h.at[pl.ds(0, rows), col(k)], near_h.at[pl.ds(rows, rows), col(k)], ps.at[k], pr.at[k], partner)

        for k in range(STEPS):
            cols = slice(k * blk, (k + 1) * blk)
            gain = refs['ln_gain'][ln_row // 2, ln_row % 2:ln_row % 2 + 1, cols].astype(F32)
            bias = refs['ln_bias'][ln_row // 2, ln_row % 2:ln_row % 2 + 1, cols].astype(F32)
            normed = (xbuf[:, cols].astype(F32) - mean) * inv
            near_h[0:rows, cols] = (normed * (1.0 + gain) + bias).astype(BF)
            if k:
                c_copy(k - 1).start()
                p_copy(k - 1).start()
        acc[:, 0:n_out] = jnp.zeros((2 * rows, n_out), F32)
        c_copy(STEPS - 1).start()
        p_copy(STEPS - 1).start()
        ready()
        for k in range(STEPS):
            p_copy(k).wait_recv()

        n_blk = n_out // STEPS
        piece = min(1024, n_out)

        def far_dot(k, cols):
            return jnp.dot(far_h[:, col(k)], wbuf[col(k), w_at + cols.start:w_at + cols.stop], preferred_element_type=F32)

        def near_step(i):
            at = pl.ds(pl.multiple_of(w_at + i * n_blk, n_blk), n_blk)
            finish(0, col(i, n_blk), jnp.dot(near_h[...], wbuf[:, at], preferred_element_type=F32), [i])
            c_copy(i).wait_recv()
            f_copy(i).start()

        def step(i, carry):
            near_step(i)
            f_copy(i - 1).wait_recv()
            for n in range(n_out // piece):
                cols = slice(n * piece, (n + 1) * piece)
                acc[:, cols] += far_dot(i - 1, cols)
            return carry

        near_step(0)
        lax.fori_loop(1, STEPS, step, 0)
        f_copy(STEPS - 1).wait_recv()
        for n in range(n_out // piece):
            cols = slice(n * piece, (n + 1) * piece)
            finish(2, cols, acc[:, cols] + far_dot(STEPS - 1, cols), range(n * piece // n_blk, (n + 1) * piece // n_blk))
        for k in range(STEPS):
            c_copy(k).wait_send()
            p_copy(k).wait_send()
            f_copy(k).wait_send()

    def split(value):
        return value.reshape(2, n_seq, toks, value.shape[-1])

    def gather_qkv(layer, total, w_at, start_now):
        stage, y_out = refs['stage'], refs['y_out']
        n_out = y_out.shape[3]
        n_blk = n_out // STEPS

        def y_copy(g, n):
            return pltpu.make_async_copy(stage.at[g, :, :, col(n, n_blk)], y_out.at[:, order[g], :, col(n, n_blk)], refs['y_sem'].at[g, n])

        def ready():
            for copy in qkv_copies(layer, w_at):
                copy.wait()

        def finish(g, cols, value, blocks):
            stage[g:g + 2, :, :, cols] = split(value)
            for n in blocks:
                y_copy(g, n).start()
                y_copy(g + 1, n).start()

        gather('g2', 2 * layer, total, w_at, n_out, ready, finish)
        for g in range(4):
            for n in range(STEPS):
                y_copy(g, n).wait()

    def qkv_copies(layer, w_at):
        copies = []
        for i, name in enumerate(('w_q', 'w_k', 'w_v')):
            width = refs[name].shape[2]
            copies.append(pltpu.make_async_copy(refs[name].at[layer], wbuf.at[:, pl.ds(w_at, width)], refs['gw_sem'].at[i]))
            w_at += width
        return copies

    x_copy = pltpu.make_async_copy(refs['x_hbm'], xbuf, refs['x_sem'])
    if cfg['first']:
        x_copy.start()
        x_copy.wait()
        for copy in qkv_copies(0, 0):
            copy.start()
        total = jnp.zeros((rows, 128), F32)
        for n in range(STEPS):
            total = fold(xbuf[:, n * blk:(n + 1) * blk].astype(F32), total)
        pl.semaphore_wait(barrier, 2)
        gather_qkv(0, total, 0, True)
        return

    layer = cfg['layer']
    abuf, act = refs['abuf'], refs['act']
    depth = abuf.shape[3]
    a_copies = [pltpu.make_async_copy(refs['a_hbm'].at[:, order[g]], abuf.at[g], refs['a_sem'].at[g]) for g in range(4)]

    def o_copy(n):
        return pltpu.make_async_copy(refs['w_o'].at[layer, :, col(n)], wbuf.at[pl.ds(0, depth), col(n)], refs['ow_sem'].at[n])

    def up_copy(i):
        span = pl.ds(0, depth) if i else pl.ds(depth, d_model - depth)
        return pltpu.make_async_copy(refs['w_up'].at[layer, span, :], wbuf.at[span, pl.ds(0, d_model)], refs['uw_sem'].at[i])

    def down_slot(n):
        return lax.rem(n + STEPS, WIDE)

    def down_copy(n):
        return pltpu.make_async_copy(refs['w_down'].at[layer, :, col(n)], wbuf.at[:, col(down_slot(n))], refs['dw_sem'].at[n])

    for g in (2, 3):
        a_copies[g].start()
    o_copy(0).start()
    for g in (0, 1):
        a_copies[g].start()
    o_copy(1).start()
    o_copy(2).start()
    x_copy.start()
    pl.semaphore_wait(barrier, 2)
    for copy in a_copies:
        copy.wait()

    def late_up(i):
        up_copy(i).start()
        if i:
            x_copy.wait()

    total = scatter('s1', abuf, o_copy, lambda n: n, depth, 3, late_up)

    def ready_up():
        for i in range(2):
            up_copy(i).wait()
        for n in range(WIDE - STEPS):
            down_copy(n).start()

    def finish_up(g, cols, value, blocks):
        act[g:g + 2, :, :, cols] = split(jnp.square(jnp.maximum(value, 0.0)).astype(BF))

    gather('g1', 2 * layer + 1, total, 0, d_model, ready_up, finish_up)

    w_at = (WIDE * blk) - (4 * blk)

    def late_qkv(i):
        if i == 0 and cfg['more']:
            for copy in qkv_copies(layer + 1, w_at):
                copy.start()

    total = scatter('s2', act, down_copy, down_slot, d_model, WIDE - STEPS, late_qkv)
    out_copy = pltpu.make_async_copy(xbuf, refs['x_out'], refs['x_sem'])
    out_copy.start()
    if cfg['more']:
        gather_qkv(layer + 1, total, w_at, False)
    out_copy.wait()


def exchange(cid, x, ln_gain, ln_bias, qkv_weights, *, n_seq, layer=-1, more=True, a=None, weights=()):
    rows, d_model = x.shape
    toks = rows // n_seq
    blk = d_model // STEPS
    first = a is None
    any_spec, vmem = pl.BlockSpec(memory_space=pl.ANY), pl.BlockSpec(memory_space=pltpu.VMEM)
    dma = pltpu.SemaphoreType.DMA
    ins = [('x_hbm', x, any_spec), ('ln_gain', ln_gain, vmem), ('ln_bias', ln_bias, vmem)]
    outs = []
    qkv_out = sum(w.shape[2] for w in qkv_weights)
    width = qkv_out if first else WIDE * blk
    scr = [('wbuf', pltpu.VMEM((d_model, width), BF)), ('xbuf', pltpu.VMEM((rows, d_model), BF)), ('x_sem', dma)]
    scr += [
        ('near_h', pltpu.VMEM((2 * rows, d_model), BF)), ('far_h', pltpu.VMEM((2 * rows, d_model), BF)),
        ('acc', pltpu.VMEM((2 * rows, qkv_out if first else d_model), F32)),
    ]
    gather_tags, flops, moved = [], 0, 4_000_000
    if not first:
        w_o, w_up, w_down = weights
        depth = a.shape[3]
        ins += [('a_hbm', a, any_spec), ('w_o', w_o, any_spec), ('w_up', w_up, any_spec), ('w_down', w_down, any_spec)]
        outs += [('x_out', jax.ShapeDtypeStruct(x.shape, BF))]
        scr += [
            ('abuf', pltpu.VMEM((4, n_seq, toks, depth), BF)), ('act', pltpu.VMEM((4, n_seq, toks, d_model), BF)),
            ('dsend', pltpu.VMEM((STEPS, 2, rows, blk), BF)), ('drecv', pltpu.VMEM((STEPS, 2, rows, blk), BF)),
            ('qsend', pltpu.VMEM((STEPS, rows, blk), BF)), ('qrecv', pltpu.VMEM((STEPS, rows, blk), BF)),
            ('own', pltpu.VMEM((STEPS, rows, blk), F32)), ('part', pltpu.VMEM((rows, blk), F32)),
            ('a_sem', dma((4,))), ('ow_sem', dma((STEPS,))), ('uw_sem', dma((2,))), ('dw_sem', dma((STEPS,))),
        ]
        for tag in ('s1', 's2'):
            scr += [(tag + k, dma((STEPS, 2))) for k in ('ds', 'dr')] + [(tag + k, dma((STEPS,))) for k in ('qs', 'qr')]
        gather_tags.append('g1')
        flops += 2 * 4 * rows * d_model * (depth + 2 * d_model)
        moved += 2 * d_model * (depth + 2 * d_model)
    if more:
        ins += list(zip(('w_q', 'w_k', 'w_v'), qkv_weights, [any_spec] * 3))
        outs += [('y_out', jax.ShapeDtypeStruct((n_seq, 4, toks, qkv_out), F32))]
        scr += [('stage', pltpu.VMEM((4, n_seq, toks, qkv_out), F32)), ('gw_sem', dma((3,))), ('y_sem', dma((4, STEPS)))]
        gather_tags.append('g2')
        flops += 2 * 4 * rows * d_model * qkv_out
        moved += 2 * d_model * qkv_out
    for tag in gather_tags:
        scr += [(tag + k, dma((STEPS,))) for k in ('cs', 'cr', 'fs', 'fr', 'ps', 'pr')]
    cfg = dict(names=[i[0] for i in ins] + [o[0] for o in outs] + [s[0] for s in scr], layer=layer, first=first, more=more, n_seq=n_seq, toks=toks, d_model=d_model)
    return pl.pallas_call(
        functools.partial(exchange_kernel, cfg),
        in_specs=[i[2] for i in ins],
        out_specs=[any_spec] * len(outs),
        out_shape=[o[1] for o in outs],
        scratch_shapes=[s[1] for s in scr],
        compiler_params=pltpu.CompilerParams(collective_id=cid, has_side_effects=True, vmem_limit_bytes=67_000_000),
        cost_estimate=pl.CostEstimate(flops=flops, bytes_accessed=moved, transcendentals=0),
        name='gather_first' if first else 'block' if more else 'block_last',
    )(*[i[1] for i in ins])


def solution(mesh):
    tok_spec = P('dp', 'tp', None)
    cache_spec = P(None, 'dp', 'tp', None, None)
    col_spec = P(None, None, 'tp')
    row_spec = P(None, 'tp', None)

    def device_fn(x_loc, start_pos, k_cache, v_cache, w_q, w_k, w_v, w_o, w_up, w_down, ln_gain, ln_bias):
        n_layers = w_q.shape[0]
        n_seq, tok_loc, d_model = x_loc.shape
        new_len = tok_loc * 4
        rows = n_seq * new_len
        positions = (start_pos[:, None] + jnp.arange(new_len, dtype=jnp.int32)[None, :]).reshape(rows)
        tabs = rope_tables(positions, k_cache.shape[4])
        hidden = x_loc.reshape(n_seq * tok_loc, d_model)
        prev = ()
        qkv_weights = (w_q, w_k, w_v)
        qkv, = exchange(0, hidden, ln_gain, ln_bias, qkv_weights, n_seq=n_seq)
        for layer in range(n_layers):
            context, *prev = attend(layer, qkv.reshape(rows, -1), tabs, start_pos, k_cache, v_cache, prev)
            context = context.reshape(n_seq, 4, tok_loc, -1)
            outs = exchange(layer + 1, hidden, ln_gain, ln_bias, qkv_weights, n_seq=n_seq, layer=layer, more=layer + 1 < n_layers, a=context, weights=(w_o, w_up, w_down))
            hidden, qkv = outs if layer + 1 < n_layers else (outs[0], None)
        return hidden.reshape(x_loc.shape), prev[0], prev[1]

    return jax.shard_map(device_fn, mesh=mesh, in_specs=(tok_spec, P('dp'), cache_spec, cache_spec, col_spec, col_spec, col_spec, row_spec, col_spec, row_spec, P(), P()), out_specs=(tok_spec, cache_spec, cache_spec), check_vma=False)
```

time: 263 us -> 253 us (0.962)
  Pallas kernels: 256 us -> 247 us
    pallas_call x5 -> x3, Pallas kernels: 203 us -> 190 us  [exchange(): pl.pallas_call(functools.partial(exchange_kernel, cfg), in_specs=[i[2] fo...]
    pallas_call x2, Pallas kernels: 52.9 us -> 57 us  [attend(): pl.pallas_call(functools.partial(attn_kernel, layer, dims), grid_spec=plt...]
where the time goes in v1:
time: 253 us; the launch traced here: 252 us
  Pallas kernels  247 us (98%)
    pallas_call x3, Pallas kernels, exchange(): pl.pallas_call(functools.partial(exchange_kernel, cfg), in_specs=[i[2] fo...  190 us
    pallas_call x2, Pallas kernels, attend(): pl.pallas_call(functools.partial(attn_kernel, layer, dims), grid_spec=plt...  57 us

profile of v1, /device:TPU:0, one launch (start us, length us, event | category | flops | bytes accessed | tf_op | source)
XLA Modules:
  0.0 252.3 jit_solution(7905918841705482378)
XLA Ops:
  0.7 0.7 add_convert_fusion
  1.4 0.1 convert_element_type.18
  1.5 0.8 fusion.3
  2.3 0.9 pad_maximum_fusion.tab_ref
  3.1 27.4 %gather_first.1 = f32[6,4,16,2048]{3,2,1,0:T(8,128)} custom-call(bf16[96,4096]{1,0:T(8,128)(2,1)} %bitcast.13, bf16[2,2,4096]{2,1,0:T(2,128)(2,1)} %args_1_.8, bf16[2,2,4096]{2,1,0:T(2,128)(2,1)} %args_2_.8, bf16[2,4096,1536]{2,1,0:T(8,128)(2,1)} %args_7_.4, bf16[2,4096,256]{2,1,0:T(8,128)(2,1)} %args_8_.4, bf16[2,4096,256]{2,1,0:T(8,128)(2,1)} %args_9_.4), custom_call_target="tpu_custom_call" | custom-call | flops 6442450944 | bytes 20777216 | tf_op jit(solution)/shard_map/gather_first/pallas_call | solution.py:529
  30.5 28.5 %attend.2 = (bf16[384,1536]{1,0:T(8,128)(2,1)}, bf16[2,6,2,3136,128]{4,3,2,1,0:T(8,128)(2,1)}, bf16[2,6,2,3136,128]{4,3,2,1,0:T(8,128)(2,1)}) custom-call(s32[6]{0:T(128)} %start_ref.3, f32[384,2048]{1,0:T(8,128)} %bitcast.6, f32[384,2048]{1,0:T(8,128)} %bitcast.7, f32[384,2048]{1,0:T(8,128)} %bitcast.8, f32[3,384,128]{2,1,0:T(8,128)} %pad_maximum_fusion.tab_ref, ...), custom_call_target="tpu_custom_call" | custom-call | flops 8000000000 | bytes 80000000 | tf_op jit(solution)/shard_map/attend/pallas_call | solution.py:193
  59.0 93.9 %block.1 = (bf16[96,4096]{1,0:T(8,128)(2,1)}, f32[6,4,16,2048]{3,2,1,0:T(8,128)}) custom-call(bf16[96,4096]{1,0:T(8,128)(2,1)} %bitcast.14, bf16[2,2,4096]{2,1,0:T(2,128)(2,1)} %args_1_.8, bf16[2,2,4096]{2,1,0:T(2,128)(2,1)} %args_2_.8, bf16[6,4,16,1536]{3,2,1,0:T(8,128)(2,1)} %bitcast.15, bf16[2,1536,4096]{2,1,0:T(8,128)(2,1)} %args_4_.8, ...), custom_call_target="tpu_custom_call" | custom-call | flops 37044092928 | bytes 100468992 | tf_op jit(solution)/shard_map/block/pallas_call | solution.py:529
  152.9 28.5 %attend.3 = (bf16[384,1536]{1,0:T(8,128)(2,1)}, bf16[2,6,2,3136,128]{4,3,2,1,0:T(8,128)(2,1)}, bf16[2,6,2,3136,128]{4,3,2,1,0:T(8,128)(2,1)}) custom-call(s32[6]{0:T(128)} %start_ref.3, f32[384,2048]{1,0:T(8,128)} %bitcast.9, f32[384,2048]{1,0:T(8,128)} %bitcast.10, f32[384,2048]{1,0:T(8,128)} %bitcast.11, ...), custom_call_target="tpu_custom_call", output_to_operand_aliasing={{1}: (7, {}), {2}: (8, {})} | custom-call | flops 8000000000 | bytes 80000000 | tf_op jit(solution)/shard_map/attend/pallas_call | solution.py:193
  181.5 68.7 %block_last.1 = bf16[96,4096]{1,0:T(8,128)(2,1)} custom-call(bf16[96,4096]{1,0:T(8,128)(2,1)} %get-tuple-element.12.args_0_, bf16[2,2,4096]{2,1,0:T(2,128)(2,1)} %args_1_.8, bf16[2,2,4096]{2,1,0:T(2,128)(2,1)} %args_2_.8, bf16[6,4,16,1536]{3,2,1,0:T(8,128)(2,1)} %bitcast.16, bf16[2,1536,4096]{2,1,0:T(8,128)(2,1)} %args_4_.8, bf16[2,4096,4096]{2,1,0:T(8,128)(2,1)} %args_5_.8, ...), custom_call_target="tpu_custom_call" | custom-call | flops 30601641984 | bytes 83691776 | tf_op jit(solution)/shard_map/block_last/pallas_call | solution.py:529
  250.2 2.1 copy.20
  (3 shorter events, 0.0 us)

commit v2 on v1

--- a/solution.py
+++ b/solution.py
@@ -16,163 +16,168 @@
 F32 = jnp.float32
 
 
-def rope_tables(positions, head_dim):
+def rope_tables(start_pos, toks, head_dim):
     rot = head_dim // 2
     half = rot // 2
-    lane = jnp.arange(head_dim, dtype=jnp.int32)
-    freq = ROPE_BASE ** (-((lane % half).astype(F32) * (2.0 / rot)))
-    angles = positions.astype(F32)[:, None] * freq
+    shape = (start_pos.shape[0], toks, head_dim)
+    lane = lax.broadcasted_iota(jnp.int32, shape, 2)
+    position = start_pos[:, None, None] + lax.broadcasted_iota(jnp.int32, shape, 1)
+    angles = position.astype(F32) * ROPE_BASE ** (-((lane % half).astype(F32) * (2.0 / rot)))
     cos_a, sin_a = jnp.cos(angles), jnp.sin(angles)
-    c_tab = jnp.where(lane < rot, cos_a, 1.0)
-    s_up = jnp.where((lane >= half) & (lane < rot), sin_a, 0.0)
-    s_dn = jnp.where(lane < half, -sin_a, 0.0)
-    return jnp.stack([c_tab, s_up, s_dn])
-
-
-def attn_kernel(layer, dims, start_ref, q_ref, k_ref, v_ref, tab_ref, kc_hbm, vc_hbm, *rest):
-    kv, group, toks, hd, s_len, ch, n_ch = dims
+    return [jnp.where(lane < rot, cos_a, 1.0), jnp.where((lane >= half) & (lane < rot), sin_a, 0.0), jnp.where(lane < half, -sin_a, 0.0)]
+
+
+def attn_kernel(layer, dims, start_ref, q_ref, k_ref, v_ref, c_ref, up_ref, dn_ref, kc_hbm, vc_hbm, *rest):
+    kv, group, toks, hd, s_len, ch = dims
     if layer > 0:
         rest = rest[2:]
     ctx_ref, ko_hbm, vo_hbm, kbuf, vbuf, sbuf, ebuf, qbuf, mbuf, pbuf, lbuf, abuf, in_sem, out_sem = rest
     b = pl.program_id(0)
-    nb = pl.num_programs(0)
-    slot = lax.rem(b, 2)
-    other = 1 - slot
+    nb = pl.num_programs(0) - 1
     s_pad = kbuf.shape[2]
     win = toks + 16
     rows = group * toks
     coef = (hd ** -0.5) * math.log2(math.e)
-
-    def load(bb, sl, go):
-        for i, (src, dst) in enumerate(((kc_hbm, kbuf), (vc_hbm, vbuf))):
-            copy = pltpu.make_async_copy(src.at[layer, bb], dst.at[sl, :, pl.ds(0, s_len), :], in_sem.at[sl, i])
-            copy.start() if go else copy.wait()
-
-    def save(bb, sl, go):
-        for i, (src, dst) in enumerate(((kbuf, ko_hbm), (vbuf, vo_hbm))):
-            copy = pltpu.make_async_copy(src.at[sl, :, pl.ds(0, s_len), :], dst.at[layer, bb], out_sem.at[sl, i])
+    slot = lax.rem(b, 3)
+    before = lax.rem(b + 2, 3)
+
+    def load(bb):
+        sl = lax.rem(bb, 3)
+        return [pltpu.make_async_copy(src.at[layer, bb], dst.at[sl, :, pl.ds(0, s_len), :], in_sem.at[sl, i]) for i, (src, dst) in enumerate(((kc_hbm, kbuf), (vc_hbm, vbuf)))]
+
+    def save(bb):
+        sl = lax.rem(bb, 3)
+        return [pltpu.make_async_copy(src.at[sl, :, pl.ds(0, s_len), :], dst.at[layer, bb], out_sem.at[sl, i]) for i, (src, dst) in enumerate(((kbuf, ko_hbm), (vbuf, vo_hbm)))]
+
+    def run(copies, go):
+        for copy in copies:
             copy.start() if go else copy.wait()
 
     @pl.when(b == 0)
     def _():
-        load(b, slot, True)
+        run(load(b), True)
         if s_pad > s_len:
-            for sl in range(2):
+            for sl in range(3):
                 kbuf[sl, :, s_len:, :] = jnp.zeros((kv, s_pad - s_len, hd), BF)
                 vbuf[sl, :, s_len:, :] = jnp.zeros((kv, s_pad - s_len, hd), BF)
 
-    @pl.when(b > 0)
+    @pl.when(b >= 2)
     def _():
-        save(b - 1, other, False)
+        run(save(b - 2), False)
 
     @pl.when(b + 1 < nb)
     def _():
-        load(b + 1, other, True)
-
-    c_tab, s_up, s_dn = tab_ref[0], tab_ref[1], tab_ref[2]
+        run(load(b + 1), True)
+
+    start = start_ref[jnp.minimum(b, nb - 1)]
+    start_before = start_ref[jnp.maximum(b - 1, 0)]
     half = hd // 4
 
     def rope(x):
-        return x * c_tab + pltpu.roll(x, half, 1) * s_up + pltpu.roll(x, hd - half, 1) * s_dn
-
-    for h in range(kv):
-        for g in range(group):
-            j = h * group + g
-            qbuf[h, g * toks:(g + 1) * toks, :] = rope(q_ref[:, j * hd:(j + 1) * hd]).astype(BF)
-
-    start = start_ref[b]
-    base = jnp.minimum((start // 16) * 16, s_len - win)
-    shift = start - base
-    base = pl.multiple_of(base, 16)
-    row_id = lax.broadcasted_iota(jnp.int32, (win, hd), 0)
-    is_new = jnp.logical_and(row_id >= shift, row_id < shift + toks)
-
-    load(b, slot, False)
-    for h in range(kv):
-        cols = slice(h * hd, (h + 1) * hd)
-        for buf, fresh in ((kbuf, rope(k_ref[:, cols])), (vbuf, v_ref[:, cols])):
-            fresh = fresh.astype(BF).astype(F32)
-            fresh = jnp.concatenate([fresh, jnp.zeros((16, hd), F32)], axis=0)
-            fresh = pltpu.roll(fresh, shift, 0)
-            old = buf[slot, h, pl.ds(base, win), :].astype(F32)
-            buf[slot, h, pl.ds(base, win), :] = jnp.where(is_new, fresh, old).astype(BF)
-    save(b, slot, True)
-
-    lbuf[...] = jnp.zeros(lbuf.shape, F32)
-    abuf[...] = jnp.zeros(abuf.shape, F32)
-    n_full = jnp.maximum(start // ch, 1)
-    n_used = (start + toks + ch - 1) // ch
+        return x * c_ref[0] + pltpu.roll(x, half, 1) * up_ref[0] + pltpu.roll(x, hd - half, 1) * dn_ref[0]
+
+    def patch():
+        base = jnp.minimum((start // 16) * 16, s_len - win)
+        shift = start - base
+        base = pl.multiple_of(base, 16)
+        row_id = lax.broadcasted_iota(jnp.int32, (win, hd), 0)
+        is_new = jnp.logical_and(row_id >= shift, row_id < shift + toks)
+        run(load(b), False)
+        for h in range(kv):
+            cols = slice(h * hd, (h + 1) * hd)
+            for buf, fresh in ((kbuf, rope(k_ref[:, cols])), (vbuf, v_ref[:, cols])):
+                fresh = fresh.astype(BF).astype(F32)
+                fresh = jnp.concatenate([fresh, jnp.zeros((16, hd), F32)], axis=0)
+                fresh = pltpu.roll(fresh, shift, 0)
+                old = buf[slot, h, pl.ds(base, win), :].astype(F32)
+                buf[slot, h, pl.ds(base, win), :] = jnp.where(is_new, fresh, old).astype(BF)
+        run(save(b), True)
+
     step_rows = 64
     blocks = [slice(r, r + step_rows) for r in range(0, ch, step_rows)]
-    ahead = lax.broadcasted_iota(jnp.int32, (step_rows, rows), 0) - lax.rem(lax.broadcasted_iota(jnp.int32, (step_rows, rows), 1), toks)
 
     def chunk(j):
         return pl.ds(pl.multiple_of(j * ch, ch), ch)
 
-    def score(h, j):
-        sbuf[h] = lax.dot_general(kbuf[slot, h, chunk(j), :], qbuf[h], (((1,), (1,)), ((), ())), preferred_element_type=F32)
-
-    def scored(h, j, rb, masked):
-        s = sbuf[h, rb]
+    def score(h, j, masked):
+        s = lax.dot_general(kbuf[slot, h, chunk(j), :], qbuf[h], (((1,), (1,)), ((), ())), preferred_element_type=F32)
         if masked:
-            s = jnp.where(ahead <= start - j * ch - rb.start, s, NEG_BIG)
-        return s.reshape(step_rows // 8, 8, rows)
-
-    def peaks(h, j, masked):
-        top = jnp.max(scored(h, j, blocks[0], masked), axis=0)
+            ahead = lax.broadcasted_iota(jnp.int32, (ch, rows), 0) - lax.rem(lax.broadcasted_iota(jnp.int32, (ch, rows), 1), toks)
+            s = jnp.where(ahead <= start - j * ch, s, NEG_BIG)
+        sbuf[h] = s
+
+    def scored(h, rb):
+        return sbuf[h, rb].reshape(step_rows // 8, 8, rows)
+
+    def peaks(h, peak):
+        top = jnp.max(scored(h, blocks[0]), axis=0)
         for rb in blocks[1:]:
-            top = jnp.maximum(top, jnp.max(scored(h, j, rb, masked), axis=0))
-        peak = pbuf[h]
+            top = jnp.maximum(top, jnp.max(scored(h, rb), axis=0))
         mbuf[h] = peak
         pbuf[h] = jnp.maximum(peak, jnp.max(top, axis=0, keepdims=True))
 
-    def weigh(h, j, masked):
+    def weigh(h):
         peak = pbuf[h]
-        total = lbuf[h] * jnp.exp2((mbuf[h] - peak) * coef)
+        alpha = jnp.exp2((mbuf[h] - peak) * coef)
+        total = lbuf[h] * alpha
         for rb in blocks:
-            e = jnp.exp2((scored(h, j, rb, masked) - peak) * coef)
+            e = jnp.exp2((scored(h, rb) - peak) * coef)
             total = total + jnp.sum(e, axis=0)
             ebuf[h, rb] = e.reshape(step_rows, rows).astype(BF)
-        lbuf[h] = total
-
-    def mix(h, j, alpha):
-        fresh = lax.dot_general(vbuf[slot, h, chunk(j), :], ebuf[h], (((0,), (0,)), ((), ())), preferred_element_type=F32)
-        abuf[h] = (abuf[h].reshape(hd // 8, 8, rows) * alpha).reshape(hd, rows) + fresh
-
-    def rescale(h):
-        return jnp.exp2((mbuf[h] - pbuf[h]) * coef)
-
-    def step(masked_now, masked_next, j, carry):
+        return alpha, total
+
+    def mix(h, sl, j, alpha):
+        fresh = lax.dot_general(vbuf[sl, h, chunk(j), :], ebuf[h], (((0,), (0,)), ((), ())), preferred_element_type=F32)
+        return (abuf[h].reshape(hd // 8, 8, rows) * alpha).reshape(hd, rows) + fresh
+
+    def step(masked_next, j, carry):
         for h in range(kv):
-            alpha = rescale(h)
-            weigh(h, j, masked_now)
-            score(h, j + 1)
-            mix(h, j, alpha)
+            alpha, lbuf[h] = weigh(h)
+            score(h, j + 1, masked_next)
+            abuf[h] = mix(h, slot, j, alpha)
         for h in range(kv):
-            peaks(h, j + 1, masked_next)
+            peaks(h, pbuf[h])
         return carry
 
-    pbuf[...] = jnp.full(pbuf.shape, NEG_BIG, F32)
-    for h in range(kv):
-        score(h, 0)
-    for h in range(kv):
-        peaks(h, 0, ch > MIN_START)
-    last = n_used - 1
-    lax.fori_loop(0, n_full - 1, functools.partial(step, ch > MIN_START, False), 0)
-    lax.fori_loop(n_full - 1, last, functools.partial(step, True, True), 0)
-    for h in range(kv):
-        alpha = rescale(h)
-        weigh(h, last, True)
-        mix(h, last, alpha)
-    for h in range(kv):
-        ctx = (abuf[h] / jnp.sum(lbuf[h], axis=0, keepdims=True)).T.astype(BF)
-        for g in range(group):
-            j = h * group + g
-            ctx_ref[:, j * hd:(j + 1) * hd] = ctx[g * toks:(g + 1) * toks, :]
-
-    @pl.when(b == nb - 1)
+    def last_of(bb_start):
+        return (bb_start + toks + ch - 1) // ch - 1
+
+    def turn(close, open_next):
+        if open_next:
+            patch()
+            for h in range(kv):
+                for g in range(group):
+                    j = h * group + g
+                    qbuf[h, g * toks:(g + 1) * toks, :] = rope(q_ref[:, j * hd:(j + 1) * hd]).astype(BF)
+        for h in range(kv):
+            if close:
+                alpha, total = weigh(h)
+            if open_next:
+                score(h, 0, ch > MIN_START)
+            if close:
+                ctx = (mix(h, before, last_of(start_before), alpha) / jnp.sum(total, axis=0, keepdims=True)).T.astype(BF)
+                for g in range(group):
+                    j = h * group + g
+                    ctx_ref[:, j * hd:(j + 1) * hd] = ctx[g * toks:(g + 1) * toks, :]
+        if open_next:
+            for h in range(kv):
+                peaks(h, jnp.full((8, rows), NEG_BIG, F32))
+                lbuf[h] = jnp.zeros((8, rows), F32)
+                abuf[h] = jnp.zeros((hd, rows), F32)
+
+    pl.when(b == 0)(functools.partial(turn, False, True))
+    pl.when(jnp.logical_and(b > 0, b < nb))(functools.partial(turn, True, True))
+    pl.when(b == nb)(functools.partial(turn, True, False))
+
+    @pl.when(b < nb)
     def _():
-        save(b, slot, False)
+        n_full = jnp.maximum(start // ch, 1)
+        lax.fori_loop(0, n_full - 1, functools.partial(step, False), 0)
+        lax.fori_loop(n_full - 1, last_of(start), functools.partial(step, True), 0)
+
+    @pl.when(b == nb)
+    def _():
+        run(save(b - 1), False)
 
 
 def attend(layer, qkv, tabs, start_pos, k_cache, v_cache, prev):
@@ -185,26 +190,27 @@
     n_ch = -(-s_len // 640)
     ch = 128 * -(-s_len // (128 * n_ch))
     rows = group * toks
-    dims = (kv, group, toks, hd, s_len, ch, n_ch)
+    dims = (kv, group, toks, hd, s_len, ch)
     any_spec = pl.BlockSpec(memory_space=pl.ANY)
-    row_map = lambda b, *_: (b, 0)
+    now = lambda b: jnp.minimum(b, n_seq - 1)
+    tab_spec = pl.BlockSpec((1, toks, hd), lambda b, *_: (now(b), 0, 0))
     cache_shape = jax.ShapeDtypeStruct(k_cache.shape, BF)
-    args = [start_pos, qkv, qkv, qkv, tabs, k_cache, v_cache] + list(prev)
+    args = [start_pos, qkv, qkv, qkv, *tabs, k_cache, v_cache] + list(prev)
     return pl.pallas_call(
         functools.partial(attn_kernel, layer, dims),
         grid_spec=pltpu.PrefetchScalarGridSpec(
             num_scalar_prefetch=1,
-            grid=(n_seq,),
+            grid=(n_seq + 1,),
             in_specs=[
-                pl.BlockSpec((toks, q_width), row_map),
-                pl.BlockSpec((toks, kv_width), lambda b, *_: (b, group)),
-                pl.BlockSpec((toks, kv_width), lambda b, *_: (b, group + 1)),
-                pl.BlockSpec((3, toks, hd), lambda b, *_: (0, b, 0)),
+                pl.BlockSpec((toks, q_width), lambda b, *_: (now(b), 0)),
+                pl.BlockSpec((toks, kv_width), lambda b, *_: (now(b), group)),
+                pl.BlockSpec((toks, kv_width), lambda b, *_: (now(b), group + 1)),
+                tab_spec, tab_spec, tab_spec,
             ] + [any_spec] * (2 + len(prev)),
-            out_specs=[pl.BlockSpec((toks, q_width), row_map), any_spec, any_spec],
+            out_specs=[pl.BlockSpec((toks, q_width), lambda b, *_: (jnp.maximum(b - 1, 0), 0)), any_spec, any_spec],
             scratch_shapes=[
-                pltpu.VMEM((2, kv, ch * n_ch, hd), BF),
-                pltpu.VMEM((2, kv, ch * n_ch, hd), BF),
+                pltpu.VMEM((3, kv, ch * n_ch, hd), BF),
+                pltpu.VMEM((3, kv, ch * n_ch, hd), BF),
                 pltpu.VMEM((kv, ch, rows), F32),
                 pltpu.VMEM((kv, ch, rows), BF),
                 pltpu.VMEM((kv, rows, hd), BF),
@@ -212,12 +218,12 @@
                 pltpu.VMEM((kv, 8, rows), F32),
                 pltpu.VMEM((kv, 8, rows), F32),
                 pltpu.VMEM((kv, hd, rows), F32),
-                pltpu.SemaphoreType.DMA((2, 2)),
-                pltpu.SemaphoreType.DMA((2, 2)),
+                pltpu.SemaphoreType.DMA((3, 2)),
+                pltpu.SemaphoreType.DMA((3, 2)),
             ],
         ),
         out_shape=[jax.ShapeDtypeStruct((n_seq * toks, q_width), BF), cache_shape, cache_shape],
-        input_output_aliases={7: 1, 8: 2} if prev else {},
+        input_output_aliases={9: 1, 10: 2} if prev else {},
         compiler_params=pltpu.CompilerParams(vmem_limit_bytes=60 * 1024 * 1024, dimension_semantics=("arbitrary",)),
         cost_estimate=pl.CostEstimate(flops=8_000_000_000, bytes_accessed=80_000_000, transcendentals=15_000_000),
         name="attend",
@@ -256,7 +262,7 @@
             total = total + values[:, j * 128:(j + 1) * 128]
         return total
 
-    def scatter(tag, a_ref, w_copy, slot_of, depth, ahead, late):
+    def scatter(tag, a_ref, w_copy, slot_of, depth, ahead, late, add=True):
         dsend, drecv, qsend, qrecv, own, part = (refs[k] for k in ('dsend', 'drecv', 'qsend', 'qrecv', 'own', 'part'))
         ds_sem, dr_sem, qs_sem, qr_sem = (refs[tag + k] for k in ('ds', 'dr', 'qs', 'qr'))
 
@@ -297,6 +303,9 @@
             d_copy(n, 1).wait_recv()
             q_copy(n).wait_recv()
             summed = own[n] + drecv[n, 1].astype(F32) + qrecv[n].astype(F32)
+            if not add:
+                xbuf[:, cols] = summed.astype(BF)
+                continue
             fresh = (xbuf[:, cols].astype(F32) + summed.astype(BF).astype(F32)).astype(BF)
             xbuf[:, cols] = fresh
             total = fold(fresh.astype(F32), total)
@@ -465,6 +474,9 @@
     def finish_up(g, cols, value, blocks):
         act[g:g + 2, :, :, cols] = split(jnp.square(jnp.maximum(value, 0.0)).astype(BF))
 
+    if not cfg['more']:
+        mid_copy = pltpu.make_async_copy(xbuf, refs['x_mid'], refs['x_sem'])
+        mid_copy.start()
     gather('g1', 2 * layer + 1, total, 0, d_model, ready_up, finish_up)
 
     w_at = (WIDE * blk) - (4 * blk)
@@ -474,7 +486,9 @@
             for copy in qkv_copies(layer + 1, w_at):
                 copy.start()
 
-    total = scatter('s2', act, down_copy, down_slot, d_model, WIDE - STEPS, late_qkv)
+    if not cfg['more']:
+        mid_copy.wait()
+    total = scatter('s2', act, down_copy, down_slot, d_model, WIDE - STEPS, late_qkv, cfg['more'])
     out_copy = pltpu.make_async_copy(xbuf, refs['x_out'], refs['x_sem'])
     out_copy.start()
     if cfg['more']:
@@ -513,6 +527,8 @@
         ]
         for tag in ('s1', 's2'):
             scr += [(tag + k, dma((STEPS, 2))) for k in ('ds', 'dr')] + [(tag + k, dma((STEPS,))) for k in ('qs', 'qr')]
+        if not more:
+            outs += [('x_mid', jax.ShapeDtypeStruct(x.shape, BF))]
         gather_tags.append('g1')
         flops += 2 * 4 * rows * d_model * (depth + 2 * d_model)
         moved += 2 * d_model * (depth + 2 * d_model)
@@ -549,8 +565,7 @@
         n_seq, tok_loc, d_model = x_loc.shape
         new_len = tok_loc * 4
         rows = n_seq * new_len
-        positions = (start_pos[:, None] + jnp.arange(new_len, dtype=jnp.int32)[None, :]).reshape(rows)
-        tabs = rope_tables(positions, k_cache.shape[4])
+        tabs = rope_tables(start_pos, new_len, k_cache.shape[4])
         hidden = x_loc.reshape(n_seq * tok_loc, d_model)
         prev = ()
         qkv_weights = (w_q, w_k, w_v)
@@ -559,7 +574,10 @@
             context, *prev = attend(layer, qkv.reshape(rows, -1), tabs, start_pos, k_cache, v_cache, prev)
             context = context.reshape(n_seq, 4, tok_loc, -1)
             outs = exchange(layer + 1, hidden, ln_gain, ln_bias, qkv_weights, n_seq=n_seq, layer=layer, more=layer + 1 < n_layers, a=context, weights=(w_o, w_up, w_down))
-            hidden, qkv = outs if layer + 1 < n_layers else (outs[0], None)
+            if layer + 1 < n_layers:
+                hidden, qkv = outs
+            else:
+                hidden = (outs[1].astype(F32) + outs[0].astype(F32)).astype(BF)
         return hidden.reshape(x_loc.shape), prev[0], prev[1]
 
     return jax.shard_map(device_fn, mesh=mesh, in_specs=(tok_spec, P('dp'), cache_spec, cache_spec, col_spec, col_spec, col_spec, row_spec, col_spec, row_spec, P(), P()), out_specs=(tok_spec, cache_spec, cache_spec), check_vma=False)

time: 253 us -> 250 us (0.988)
  Pallas kernels: 247 us -> 241 us
    pallas_call x2, Pallas kernels: 57 us -> 51.6 us  [attend(): pl.pallas_call(functools.partial(attn_kernel, layer, dims), grid_spec=plt...]
where the time goes in v2:
time: 250 us; the launch traced here: 247 us
  Pallas kernels  241 us (96%)
  other arithmetic  4.68 us (2%)
    pallas_call x3, Pallas kernels, exchange(): pl.pallas_call(functools.partial(exchange_kernel, cfg), in_specs=[i[2] fo...  190 us
    pallas_call x2, Pallas kernels, attend(): pl.pallas_call(functools.partial(attn_kernel, layer, dims), grid_spec=plt...  51.6 us

profile of v2, /device:TPU:0, one launch (start us, length us, event | category | flops | bytes accessed | tf_op | source)
XLA Modules:
  0.0 246.8 jit_solution(9156000549059048596)
XLA Ops:
  0.7 2.2 negate_select_fusion
  2.9 27.4 %gather_first.1 = f32[6,4,16,2048]{3,2,1,0:T(8,128)} custom-call(bf16[96,4096]{1,0:T(8,128)(2,1)} %bitcast.12, bf16[2,2,4096]{2,1,0:T(2,128)(2,1)} %args_1_.8, bf16[2,2,4096]{2,1,0:T(2,128)(2,1)} %args_2_.8, bf16[2,4096,1536]{2,1,0:T(8,128)(2,1)} %args_7_.4, bf16[2,4096,256]{2,1,0:T(8,128)(2,1)} %args_8_.4, bf16[2,4096,256]{2,1,0:T(8,128)(2,1)} %args_9_.4), custom_call_target="tpu_custom_call" | custom-call | flops 6442450944 | bytes 20777216 | tf_op jit(solution)/shard_map/gather_first/pallas_call | solution.py:545
  30.2 25.8 %attend.2 = (bf16[384,1536]{1,0:T(8,128)(2,1)}, bf16[2,6,2,3136,128]{4,3,2,1,0:T(8,128)(2,1)}, bf16[2,6,2,3136,128]{4,3,2,1,0:T(8,128)(2,1)}) custom-call(s32[6]{0:T(128)} %start_ref.3, f32[384,2048]{1,0:T(8,128)} %bitcast.6, f32[384,2048]{1,0:T(8,128)} %bitcast.7, f32[384,2048]{1,0:T(8,128)} %bitcast.8, f32[6,64,128]{2,1,0:T(8,128)} %get-tuple-element.24.c_ref, ...), custom_call_target="tpu_custom_call" | custom-call | flops 8000000000 | bytes 80000000 | tf_op jit(solution)/shard_map/attend/pallas_call | solution.py:199
  56.1 93.9 %block.1 = (bf16[96,4096]{1,0:T(8,128)(2,1)}, f32[6,4,16,2048]{3,2,1,0:T(8,128)}) custom-call(bf16[96,4096]{1,0:T(8,128)(2,1)} %bitcast.13, bf16[2,2,4096]{2,1,0:T(2,128)(2,1)} %args_1_.8, bf16[2,2,4096]{2,1,0:T(2,128)(2,1)} %args_2_.8, bf16[6,4,16,1536]{3,2,1,0:T(8,128)(2,1)} %bitcast.14, bf16[2,1536,4096]{2,1,0:T(8,128)(2,1)} %args_4_.8, ...), custom_call_target="tpu_custom_call" | custom-call | flops 37044092928 | bytes 100468992 | tf_op jit(solution)/shard_map/block/pallas_call | solution.py:545
  149.9 25.8 %attend.3 = (bf16[384,1536]{1,0:T(8,128)(2,1)}, bf16[2,6,2,3136,128]{4,3,2,1,0:T(8,128)(2,1)}, bf16[2,6,2,3136,128]{4,3,2,1,0:T(8,128)(2,1)}) custom-call(s32[6]{0:T(128)} %start_ref.3, f32[384,2048]{1,0:T(8,128)} %bitcast.9, f32[384,2048]{1,0:T(8,128)} %bitcast.10, f32[384,2048]{1,0:T(8,128)} %bitcast.11, ...), custom_call_target="tpu_custom_call", output_to_operand_aliasing={{1}: (9, {}), {2}: (10, {})} | custom-call | flops 8000000000 | bytes 80000000 | tf_op jit(solution)/shard_map/attend/pallas_call | solution.py:199
  175.7 68.6 %block_last.1 = (bf16[96,4096]{1,0:T(8,128)(2,1)}, bf16[96,4096]{1,0:T(8,128)(2,1)}) custom-call(bf16[96,4096]{1,0:T(8,128)(2,1)} %get-tuple-element.14.args_0_, bf16[2,2,4096]{2,1,0:T(2,128)(2,1)} %args_1_.8, bf16[2,2,4096]{2,1,0:T(2,128)(2,1)} %args_2_.8, bf16[6,4,16,1536]{3,2,1,0:T(8,128)(2,1)} %bitcast.15, bf16[2,1536,4096]{2,1,0:T(8,128)(2,1)} %args_4_.8, ...), custom_call_target="tpu_custom_call" | custom-call | flops 30601641984 | bytes 83691776 | tf_op jit(solution)/shard_map/block_last/pallas_call | solution.py:545
  244.3 2.4 add_convert_fusion
  (3 shorter events, 0.0 us)

commit v3 on v2

--- a/solution.py
+++ b/solution.py
@@ -12,22 +12,25 @@
 ROPE_BASE = 10000.0
 NEG_BIG = -1e30
 MIN_START = 768
+SLOTS = 4
 BF = jnp.bfloat16
 F32 = jnp.float32
 
 
-def rope_tables(start_pos, toks, head_dim):
+def rope_tables(start, toks, head_dim):
     rot = head_dim // 2
     half = rot // 2
-    shape = (start_pos.shape[0], toks, head_dim)
-    lane = lax.broadcasted_iota(jnp.int32, shape, 2)
-    position = start_pos[:, None, None] + lax.broadcasted_iota(jnp.int32, shape, 1)
-    angles = position.astype(F32) * ROPE_BASE ** (-((lane % half).astype(F32) * (2.0 / rot)))
+    shape = (toks, head_dim)
+    lane = lax.broadcasted_iota(jnp.int32, shape, 1)
+    position = start + lax.broadcasted_iota(jnp.int32, shape, 0)
+    power = lax.rem(lane, half).astype(F32) * (2.0 / rot)
+    angles = position.astype(F32) * jnp.exp(power * -math.log(ROPE_BASE))
     cos_a, sin_a = jnp.cos(angles), jnp.sin(angles)
-    return [jnp.where(lane < rot, cos_a, 1.0), jnp.where((lane >= half) & (lane < rot), sin_a, 0.0), jnp.where(lane < half, -sin_a, 0.0)]
-
-
-def attn_kernel(layer, dims, start_ref, q_ref, k_ref, v_ref, c_ref, up_ref, dn_ref, kc_hbm, vc_hbm, *rest):
+    upper = jnp.logical_and(lane >= half, lane < rot)
+    return jnp.where(lane < rot, cos_a, 1.0), jnp.where(upper, sin_a, 0.0), jnp.where(lane < half, -sin_a, 0.0)
+
+
+def attn_kernel(layer, dims, start_ref, q_ref, k_ref, v_ref, tab_ref, kc_hbm, vc_hbm, *rest):
     kv, group, toks, hd, s_len, ch = dims
     if layer > 0:
         rest = rest[2:]
@@ -38,15 +41,15 @@
     win = toks + 16
     rows = group * toks
     coef = (hd ** -0.5) * math.log2(math.e)
-    slot = lax.rem(b, 3)
-    before = lax.rem(b + 2, 3)
+    slot = lax.rem(b, SLOTS)
+    before = lax.rem(b + SLOTS - 1, SLOTS)
 
     def load(bb):
-        sl = lax.rem(bb, 3)
+        sl = lax.rem(bb, SLOTS)
         return [pltpu.make_async_copy(src.at[layer, bb], dst.at[sl, :, pl.ds(0, s_len), :], in_sem.at[sl, i]) for i, (src, dst) in enumerate(((kc_hbm, kbuf), (vc_hbm, vbuf)))]
 
     def save(bb):
-        sl = lax.rem(bb, 3)
+        sl = lax.rem(bb, SLOTS)
         return [pltpu.make_async_copy(src.at[sl, :, pl.ds(0, s_len), :], dst.at[layer, bb], out_sem.at[sl, i]) for i, (src, dst) in enumerate(((kbuf, ko_hbm), (vbuf, vo_hbm)))]
 
     def run(copies, go):
@@ -57,7 +60,7 @@
     def _():
         run(load(b), True)
         if s_pad > s_len:
-            for sl in range(3):
+            for sl in range(SLOTS):
                 kbuf[sl, :, s_len:, :] = jnp.zeros((kv, s_pad - s_len, hd), BF)
                 vbuf[sl, :, s_len:, :] = jnp.zeros((kv, s_pad - s_len, hd), BF)
 
@@ -65,16 +68,16 @@
     def _():
         run(save(b - 2), False)
 
-    @pl.when(b + 1 < nb)
+    @pl.when(jnp.logical_and(b > 0, b + 2 < nb))
     def _():
-        run(load(b + 1), True)
+        run(load(b + 2), True)
 
     start = start_ref[jnp.minimum(b, nb - 1)]
     start_before = start_ref[jnp.maximum(b - 1, 0)]
     half = hd // 4
 
     def rope(x):
-        return x * c_ref[0] + pltpu.roll(x, half, 1) * up_ref[0] + pltpu.roll(x, hd - half, 1) * dn_ref[0]
+        return x * tab_ref[0, 0] + pltpu.roll(x, half, 1) * tab_ref[1, 0] + pltpu.roll(x, hd - half, 1) * tab_ref[2, 0]
 
     def patch():
         base = jnp.minimum((start // 16) * 16, s_len - win)
@@ -83,6 +86,12 @@
         row_id = lax.broadcasted_iota(jnp.int32, (win, hd), 0)
         is_new = jnp.logical_and(row_id >= shift, row_id < shift + toks)
         run(load(b), False)
+
+        @pl.when(b == 0)
+        def _():
+            run(load(b + 1), True)
+            run(load(b + 2), True)
+
         for h in range(kv):
             cols = slice(h * hd, (h + 1) * hd)
             for buf, fresh in ((kbuf, rope(k_ref[:, cols])), (vbuf, v_ref[:, cols])):
@@ -193,9 +202,9 @@
     dims = (kv, group, toks, hd, s_len, ch)
     any_spec = pl.BlockSpec(memory_space=pl.ANY)
     now = lambda b: jnp.minimum(b, n_seq - 1)
-    tab_spec = pl.BlockSpec((1, toks, hd), lambda b, *_: (now(b), 0, 0))
+    tab_spec = pl.BlockSpec((3, 1, toks, hd), lambda b, *_: (0, now(b), 0, 0))
     cache_shape = jax.ShapeDtypeStruct(k_cache.shape, BF)
-    args = [start_pos, qkv, qkv, qkv, *tabs, k_cache, v_cache] + list(prev)
+    args = [start_pos, qkv, qkv, qkv, tabs, k_cache, v_cache] + list(prev)
     return pl.pallas_call(
         functools.partial(attn_kernel, layer, dims),
         grid_spec=pltpu.PrefetchScalarGridSpec(
@@ -205,12 +214,12 @@
                 pl.BlockSpec((toks, q_width), lambda b, *_: (now(b), 0)),
                 pl.BlockSpec((toks, kv_width), lambda b, *_: (now(b), group)),
                 pl.BlockSpec((toks, kv_width), lambda b, *_: (now(b), group + 1)),
-                tab_spec, tab_spec, tab_spec,
+                tab_spec,
             ] + [any_spec] * (2 + len(prev)),
             out_specs=[pl.BlockSpec((toks, q_width), lambda b, *_: (jnp.maximum(b - 1, 0), 0)), any_spec, any_spec],
             scratch_shapes=[
-                pltpu.VMEM((3, kv, ch * n_ch, hd), BF),
-                pltpu.VMEM((3, kv, ch * n_ch, hd), BF),
+                pltpu.VMEM((SLOTS, kv, ch * n_ch, hd), BF),
+                pltpu.VMEM((SLOTS, kv, ch * n_ch, hd), BF),
                 pltpu.VMEM((kv, ch, rows), F32),
                 pltpu.VMEM((kv, ch, rows), BF),
                 pltpu.VMEM((kv, rows, hd), BF),
@@ -218,12 +227,12 @@
                 pltpu.VMEM((kv, 8, rows), F32),
                 pltpu.VMEM((kv, 8, rows), F32),
                 pltpu.VMEM((kv, hd, rows), F32),
-                pltpu.SemaphoreType.DMA((3, 2)),
-                pltpu.SemaphoreType.DMA((3, 2)),
+                pltpu.SemaphoreType.DMA((SLOTS, 2)),
+                pltpu.SemaphoreType.DMA((SLOTS, 2)),
             ],
         ),
         out_shape=[jax.ShapeDtypeStruct((n_seq * toks, q_width), BF), cache_shape, cache_shape],
-        input_output_aliases={9: 1, 10: 2} if prev else {},
+        input_output_aliases={7: 1, 8: 2} if prev else {},
         compiler_params=pltpu.CompilerParams(vmem_limit_bytes=60 * 1024 * 1024, dimension_semantics=("arbitrary",)),
         cost_estimate=pl.CostEstimate(flops=8_000_000_000, bytes_accessed=80_000_000, transcendentals=15_000_000),
         name="attend",
@@ -262,7 +271,7 @@
             total = total + values[:, j * 128:(j + 1) * 128]
         return total
 
-    def scatter(tag, a_ref, w_copy, slot_of, depth, ahead, late, add=True):
+    def scatter(tag, a_ref, w_copy, slot_of, depth, ahead, late):
         dsend, drecv, qsend, qrecv, own, part = (refs[k] for k in ('dsend', 'drecv', 'qsend', 'qrecv', 'own', 'part'))
         ds_sem, dr_sem, qs_sem, qr_sem = (refs[tag + k] for k in ('ds', 'dr', 'qs', 'qr'))
 
@@ -303,9 +312,6 @@
             d_copy(n, 1).wait_recv()
             q_copy(n).wait_recv()
             summed = own[n] + drecv[n, 1].astype(F32) + qrecv[n].astype(F32)
-            if not add:
-                xbuf[:, cols] = summed.astype(BF)
-                continue
             fresh = (xbuf[:, cols].astype(F32) + summed.astype(BF).astype(F32)).astype(BF)
             xbuf[:, cols] = fresh
             total = fold(fresh.astype(F32), total)
@@ -393,6 +399,16 @@
             return pltpu.make_async_copy(stage.at[g, :, :, col(n, n_blk)], y_out.at[:, order[g], :, col(n, n_blk)], refs['y_sem'].at[g, n])
 
         def ready():
+            if start_now:
+                tabs = refs['tabs']
+
+                def table(b, carry):
+                    for i, part in enumerate(rope_tables(refs['start'][b], tabs.shape[2], tabs.shape[3])):
+                        tabs[i, b] = part
+                    return carry
+
+                lax.fori_loop(0, n_seq, table, 0)
+                tab_copy.start()
             for copy in qkv_copies(layer, w_at):
                 copy.wait()
 
@@ -402,7 +418,11 @@
                 y_copy(g, n).start()
                 y_copy(g + 1, n).start()
 
+        if start_now:
+            tab_copy = pltpu.make_async_copy(refs['tabs'], refs['tab_out'], refs['tab_sem'])
         gather('g2', 2 * layer, total, w_at, n_out, ready, finish)
+        if start_now:
+            tab_copy.wait()
         for g in range(4):
             for n in range(STEPS):
                 y_copy(g, n).wait()
@@ -474,9 +494,6 @@
     def finish_up(g, cols, value, blocks):
         act[g:g + 2, :, :, cols] = split(jnp.square(jnp.maximum(value, 0.0)).astype(BF))
 
-    if not cfg['more']:
-        mid_copy = pltpu.make_async_copy(xbuf, refs['x_mid'], refs['x_sem'])
-        mid_copy.start()
     gather('g1', 2 * layer + 1, total, 0, d_model, ready_up, finish_up)
 
     w_at = (WIDE * blk) - (4 * blk)
@@ -486,9 +503,7 @@
             for copy in qkv_copies(layer + 1, w_at):
                 copy.start()
 
-    if not cfg['more']:
-        mid_copy.wait()
-    total = scatter('s2', act, down_copy, down_slot, d_model, WIDE - STEPS, late_qkv, cfg['more'])
+    total = scatter('s2', act, down_copy, down_slot, d_model, WIDE - STEPS, late_qkv)
     out_copy = pltpu.make_async_copy(xbuf, refs['x_out'], refs['x_sem'])
     out_copy.start()
     if cfg['more']:
@@ -496,7 +511,7 @@
     out_copy.wait()
 
 
-def exchange(cid, x, ln_gain, ln_bias, qkv_weights, *, n_seq, layer=-1, more=True, a=None, weights=()):
+def exchange(cid, x, ln_gain, ln_bias, qkv_weights, *, n_seq, layer=-1, more=True, a=None, weights=(), start_pos=None, head_dim=0):
     rows, d_model = x.shape
     toks = rows // n_seq
     blk = d_model // STEPS
@@ -527,8 +542,6 @@
         ]
         for tag in ('s1', 's2'):
             scr += [(tag + k, dma((STEPS, 2))) for k in ('ds', 'dr')] + [(tag + k, dma((STEPS,))) for k in ('qs', 'qr')]
-        if not more:
-            outs += [('x_mid', jax.ShapeDtypeStruct(x.shape, BF))]
         gather_tags.append('g1')
         flops += 2 * 4 * rows * d_model * (depth + 2 * d_model)
         moved += 2 * d_model * (depth + 2 * d_model)
@@ -539,6 +552,11 @@
         gather_tags.append('g2')
         flops += 2 * 4 * rows * d_model * qkv_out
         moved += 2 * d_model * qkv_out
+    if first:
+        tab_shape = (3, n_seq, 4 * toks, head_dim)
+        ins += [('start', start_pos, pl.BlockSpec(memory_space=pltpu.SMEM))]
+        outs += [('tab_out', jax.ShapeDtypeStruct(tab_shape, F32))]
+        scr += [('tabs', pltpu.VMEM(tab_shape, F32)), ('tab_sem', dma)]
     for tag in gather_tags:
         scr += [(tag + k, dma((STEPS,))) for k in ('cs', 'cr', 'fs', 'fr', 'ps', 'pr')]
     cfg = dict(names=[i[0] for i in ins] + [o[0] for o in outs] + [s[0] for s in scr], layer=layer, first=first, more=more, n_seq=n_seq, toks=toks, d_model=d_model)
@@ -565,19 +583,15 @@
         n_seq, tok_loc, d_model = x_loc.shape
         new_len = tok_loc * 4
         rows = n_seq * new_len
-        tabs = rope_tables(start_pos, new_len, k_cache.shape[4])
         hidden = x_loc.reshape(n_seq * tok_loc, d_model)
         prev = ()
         qkv_weights = (w_q, w_k, w_v)
-        qkv, = exchange(0, hidden, ln_gain, ln_bias, qkv_weights, n_seq=n_seq)
+        qkv, tabs = exchange(0, hidden, ln_gain, ln_bias, qkv_weights, n_seq=n_seq, start_pos=start_pos, head_dim=k_cache.shape[4])
         for layer in range(n_layers):
             context, *prev = attend(layer, qkv.reshape(rows, -1), tabs, start_pos, k_cache, v_cache, prev)
             context = context.reshape(n_seq, 4, tok_loc, -1)
             outs = exchange(layer + 1, hidden, ln_gain, ln_bias, qkv_weights, n_seq=n_seq, layer=layer, more=layer + 1 < n_layers, a=context, weights=(w_o, w_up, w_down))
-            if layer + 1 < n_layers:
-                hidden, qkv = outs
-            else:
-                hidden = (outs[1].astype(F32) + outs[0].astype(F32)).astype(BF)
+            hidden, qkv = outs if layer + 1 < n_layers else (outs[0], None)
         return hidden.reshape(x_loc.shape), prev[0], prev[1]
 
     return jax.shard_map(device_fn, mesh=mesh, in_specs=(tok_spec, P('dp'), cache_spec, cache_spec, col_spec, col_spec, col_spec, row_spec, col_spec, row_spec, P(), P()), out_specs=(tok_spec, cache_spec, cache_spec), check_vma=False)

time: 250 us -> 245 us (0.980); the launches traced: 247 us -> 247 us
  other arithmetic: 4.68 us -> 0 us
  Pallas kernels: 241 us -> 244 us
    pallas_call x2, Pallas kernels: 51.6 us -> 54.6 us  [attend(): pl.pallas_call(functools.partial(attn_kernel, layer, dims), grid_spec=plt...]
where the time goes in v3:
time: 245 us; the launch traced here: 247 us
  Pallas kernels  244 us (100%)
    pallas_call x3, Pallas kernels, exchange(): pl.pallas_call(functools.partial(exchange_kernel, cfg), in_specs=[i[2] fo...  190 us
    pallas_call x2, Pallas kernels, attend(): pl.pallas_call(functools.partial(attn_kernel, layer, dims), grid_spec=plt...  54.6 us

profile of v3, /device:TPU:0, one launch (start us, length us, event | category | flops | bytes accessed | tf_op | source)
XLA Modules:
  0.0 247.2 jit_solution(13103216600095185423)
XLA Ops:
  0.6 27.4 %gather_first.1 = (f32[6,4,16,2048]{3,2,1,0:T(8,128)}, f32[3,6,64,128]{3,2,1,0:T(8,128)}) custom-call(bf16[96,4096]{1,0:T(8,128)(2,1)} %bitcast.13, bf16[2,2,4096]{2,1,0:T(2,128)(2,1)} %args_1_.8, bf16[2,2,4096]{2,1,0:T(2,128)(2,1)} %args_2_.8, bf16[2,4096,1536]{2,1,0:T(8,128)(2,1)} %args_7_.4, bf16[2,4096,256]{2,1,0:T(8,128)(2,1)} %args_8_.4, ...), custom_call_target="tpu_custom_call" | custom-call | flops 6442450944 | bytes 20777216 | tf_op jit(solution)/shard_map/gather_first/pallas_call | solution.py:563
  28.1 27.3 %attend.2 = (bf16[384,1536]{1,0:T(8,128)(2,1)}, bf16[2,6,2,3136,128]{4,3,2,1,0:T(8,128)(2,1)}, bf16[2,6,2,3136,128]{4,3,2,1,0:T(8,128)(2,1)}) custom-call(s32[6]{0:T(128)} %start_ref.3, f32[384,2048]{1,0:T(8,128)} %bitcast.9, f32[384,2048]{1,0:T(8,128)} %bitcast.10, f32[384,2048]{1,0:T(8,128)} %bitcast.11, f32[3,6,64,128]{3,2,1,0:T(8,128)} %get-tuple-element.14.tab_ref, ...), custom_call_target="tpu_custom_call" | custom-call | flops 8000000000 | bytes 80000000 | tf_op jit(solution)/shard_map/attend/pallas_call | solution.py:208
  55.4 93.8 %block.1 = (bf16[96,4096]{1,0:T(8,128)(2,1)}, f32[6,4,16,2048]{3,2,1,0:T(8,128)}) custom-call(bf16[96,4096]{1,0:T(8,128)(2,1)} %bitcast.14, bf16[2,2,4096]{2,1,0:T(2,128)(2,1)} %args_1_.8, bf16[2,2,4096]{2,1,0:T(2,128)(2,1)} %args_2_.8, bf16[6,4,16,1536]{3,2,1,0:T(8,128)(2,1)} %bitcast.15, bf16[2,1536,4096]{2,1,0:T(8,128)(2,1)} %args_4_.8, ...), custom_call_target="tpu_custom_call" | custom-call | flops 37044092928 | bytes 100468992 | tf_op jit(solution)/shard_map/block/pallas_call | solution.py:563
  149.2 27.3 %attend.3 = (bf16[384,1536]{1,0:T(8,128)(2,1)}, bf16[2,6,2,3136,128]{4,3,2,1,0:T(8,128)(2,1)}, bf16[2,6,2,3136,128]{4,3,2,1,0:T(8,128)(2,1)}) custom-call(s32[6]{0:T(128)} %start_ref.3, f32[384,2048]{1,0:T(8,128)} %bitcast.6, f32[384,2048]{1,0:T(8,128)} %bitcast.7, f32[384,2048]{1,0:T(8,128)} %bitcast.8, ...), custom_call_target="tpu_custom_call", output_to_operand_aliasing={{1}: (7, {}), {2}: (8, {})} | custom-call | flops 8000000000 | bytes 80000000 | tf_op jit(solution)/shard_map/attend/pallas_call | solution.py:208
  176.5 68.6 %block_last.1 = bf16[96,4096]{1,0:T(8,128)(2,1)} custom-call(bf16[96,4096]{1,0:T(8,128)(2,1)} %get-tuple-element.16.args_0_, bf16[2,2,4096]{2,1,0:T(2,128)(2,1)} %args_1_.8, bf16[2,2,4096]{2,1,0:T(2,128)(2,1)} %args_2_.8, bf16[6,4,16,1536]{3,2,1,0:T(8,128)(2,1)} %bitcast.16, bf16[2,1536,4096]{2,1,0:T(8,128)(2,1)} %args_4_.8, bf16[2,4096,4096]{2,1,0:T(8,128)(2,1)} %args_5_.8, ...), custom_call_target="tpu_custom_call" | custom-call | flops 30601641984 | bytes 83691776 | tf_op jit(solution)/shard_map/block_last/pallas_call | solution.py:563
  245.1 2.1 copy.20
